TPU v7x, 32 devices: a whole 2x2x4 slice. The times are simulated.
32 devices in a mesh: dp: 4 (over y, core), tensor: 2 (over x), pipe: 4 (over z).
Axes of the slice: x: 2, y: 2, z: 4, core: 2. Of those that a mesh axis runs over, the one named last changes fastest.
Arguments:
- grad_parts: float32 [4, 4, 2, 64, 8192], P('dp', 'pipe', 'tensor'), may hold values from -24 to 24
- drop_flags: int32 [4, 4, 2, 64], P('dp', 'pipe', 'tensor'), may hold values from 0 to 1, as said below
- owner_order: int32 [4], replicated, may hold values from 0 to 3, each once
- step_count: int32 [], replicated, may hold values from 1 to 11
- master: float32 [4, 2, 64, 8192], P('pipe', 'tensor', None, 'dp'), may hold values from -6 to 6
- moment_m: float32 [4, 2, 64, 8192], P('pipe', 'tensor', None, 'dp'), may hold values from -0.15625 to 0.15625
- moment_v: float32 [4, 2, 64, 8192], P('pipe', 'tensor', None, 'dp'), may hold values from 0.0001 to 0.001
Outputs:
- new_master: float32 [4, 2, 64, 8192], P('pipe', 'tensor', None, 'dp')
- new_m: float32 [4, 2, 64, 8192], P('pipe', 'tensor', None, 'dp')
- new_v: float32 [4, 2, 64, 8192], P('pipe', 'tensor', None, 'dp')
- direction: float32 [4, 2, 64, 8192], P('pipe', 'tensor', None, 'dp')
- dropped_total: int32 [], replicated
Inputs may be any that keep to these rules, and one draw needn't show every extreme that they name: `drop_flags`: A row may be flagged by every replica.
All inputs are finite; a program needn't handle non-finite values.
Results may differ from a plain program's by a relative error of at most 0.0003.
Values sent between devices are 32-bit elements; how exact they have to be, the bound alone decides.
A program may use at most 64 MiB of HBM per device.

v0:
```python
import functools
import itertools
import jax
import jax.numpy as jnp
from jax import lax
from jax.experimental import pallas as pl
from jax.experimental.pallas import tpu as pltpu
from jax.sharding import PartitionSpec as P

AXES = ("dp", "tensor", "pipe")
MESH = pl.DeviceIdType.MESH
LANES = 128
DIRECT = 64
VMEM_MOST = 67043328


def as_column(row, rows):
    square = (rows, rows)
    diagonal = lax.broadcasted_iota(jnp.int32, square, 0) == lax.broadcasted_iota(jnp.int32, square, 1)
    return jnp.sum(jnp.where(diagonal, jnp.broadcast_to(row, square), 0.0), axis=1, keepdims=True)


def int_power(base, exponent):
    result = jnp.ones(exponent.shape, jnp.float32)
    square = jnp.full(exponent.shape, base, jnp.float32)
    for bit in range(31):
        result = jnp.where((exponent >> bit) & 1 == 1, result * square, result)
        square = square * square
    return result


def kernel(
    sizes, stages, chunks,
    order_hbm, flags_hbm, grad_hbm,
    total, norm_out,
    order_ref, flags_ref, g_bufs, pair_send, pair_recv, ring_send, ring_recv,
    kept_send, kept_recv, red_sends, red_recvs,
    o_sem, g_sem, ps_sem, pr_sem, rs_sem, rr_sem, ks_sem, kr_sem, as_sems, ar_sems,
):
    n = sizes["dp"]
    chips = n // 2
    rows, width = total.shape
    part = rows // chunks
    me = {axis: lax.axis_index(axis) for axis in AXES}
    chip, core = lax.div(me["dp"], 2), lax.rem(me["dp"], 2)

    def peer(offsets):
        return {axis: lax.rem(me[axis] + off, sizes[axis]) for axis, off in offsets.items()}

    def offsets_of(axes):
        ranges = [range(sizes[axis]) for axis in axes]
        return [dict(zip(axes, offs)) for offs in itertools.product(*ranges) if any(offs)]

    small = [
        pltpu.make_async_copy(order_hbm, order_ref, o_sem.at[0]),
        pltpu.make_async_copy(flags_hbm, flags_ref, o_sem.at[1]),
    ]
    for copy in small:
        copy.start()
    loads = []
    for k in range(chunks):
        copy = pltpu.make_async_copy(grad_hbm.at[0, 0, 0, pl.ds(k * part, part)], g_bufs[k], g_sem.at[k])
        copy.start()
        loads.append(copy)

    barrier = pltpu.get_barrier_semaphore()
    friends = [tuple(sorted(off.items())) for axes in stages for off in offsets_of(axes)]
    friends += [tuple(sorted(off.items())) for off in offsets_of(("dp",))]
    full = [tuple(sorted({**dict.fromkeys(AXES, 0), **dict(off)}.items())) for off in friends]
    full = list(dict.fromkeys(full))
    for off in full:
        pl.semaphore_signal(barrier, inc=1, device_id=peer(dict(off)), device_id_type=MESH)

    for copy in small:
        copy.wait()
    flags_row = flags_ref[0].astype(jnp.float32)
    kept_row = 1.0 - flags_row
    kept = as_column(kept_row, rows)
    kept_send[0, :, 0:rows] = kept_row
    dropped = jnp.sum(flags_row, axis=1, keepdims=True)

    def chip_at(slot):
        return lax.rem(chip + slot, chips)

    def term(k, owner):
        block = order_ref[owner]
        picked = None
        for b in range(n):
            weight = (1 - jnp.minimum(jnp.maximum(block - b, b - block), 1)).astype(jnp.float32)
            piece = g_bufs[k][:, b * width:(b + 1) * width] * weight
            picked = piece if picked is None else picked + piece
        return picked * kept[k * part:(k + 1) * part]

    slots = list(range(1, chips)) + [0]
    for k in range(chunks):
        loads[k].wait()
        for slot in slots:
            pair_send[k, slot] = term(k, chip_at(slot) * 2 + 1 - core)

    pl.semaphore_wait(barrier, len(full))

    sibling = {"dp": chip * 2 + 1 - core}
    pair, waits = {}, []
    for group in (slots[:-1], slots[-1:]):
        for k in range(chunks):
            for slot in group:
                copy = pltpu.make_async_remote_copy(
                    pair_send.at[k, slot], pair_recv.at[k, slot],
                    ps_sem.at[k, slot], pr_sem.at[k, slot],
                    device_id=sibling, device_id_type=MESH,
                )
                copy.start()
                pair[k, slot] = copy
                waits.append(copy)
    kepts = []
    for off in range(1, n):
        copy = pltpu.make_async_remote_copy(
            kept_send.at[0], kept_recv.at[off - 1], ks_sem.at[off - 1], kr_sem.at[off - 1],
            device_id=peer({"dp": off}), device_id_type=MESH,
        )
        copy.start()
        kepts.append(copy)
        waits.append(copy)

    ring = {}
    for k in range(chunks):
        for slot in range(1, chips):
            target = chip_at(slot) * 2 + core
            mine = term(k, target)
            pair[k, slot].wait_recv()
            ring_send[k, slot - 1] = pair_recv[k, slot] + mine
            copy = pltpu.make_async_remote_copy(
                ring_send.at[k, slot - 1], ring_recv.at[k, slot - 1],
                rs_sem.at[k, slot - 1], rr_sem.at[k, slot - 1],
                device_id={"dp": target}, device_id_type=MESH,
            )
            copy.start()
            ring[k, slot] = copy
            waits.append(copy)

    count_row = kept_row
    for i, copy in enumerate(kepts):
        copy.wait_recv()
        count_row = count_row + kept_recv[i, :, 0:rows]
    inverse = 1.0 / jnp.maximum(as_column(count_row, rows), 1.0)

    for k in range(chunks):
        mine = term(k, me["dp"])
        pair[k, 0].wait_recv()
        total[k * part:(k + 1) * part, :] = pair_recv[k, 0] + mine

    squares = jnp.zeros((8, LANES), jnp.float32)
    for k in range(chunks):
        at = slice(k * part, (k + 1) * part)
        value = total[at, :]
        for slot in range(1, chips):
            ring[k, slot].wait_recv()
            value = value + ring_recv[k, slot - 1]
        value = value * inverse[at]
        total[at, :] = value
        squares = squares + jnp.sum(
            (value * value).reshape(part // 8, 8, width // LANES, LANES), axis=(0, 2)
        )

    lane = lax.broadcasted_iota(jnp.int32, (1, LANES), 1)
    half = LANES // 2
    packed = jnp.sum(squares, axis=0, keepdims=True)
    packed = packed + pltpu.roll(packed, half, 1)
    packed = jnp.where(lane < half, packed, jnp.where(lane == half, dropped, 0.0))
    for axes, send, recv, s_sem, r_sem in zip(stages, red_sends, red_recvs, as_sems, ar_sems):
        send[0] = packed
        copies = []
        for i, off in enumerate(offsets_of(axes)):
            copy = pltpu.make_async_remote_copy(
                send.at[0], recv.at[i], s_sem.at[i], r_sem.at[i],
                device_id=peer(off), device_id_type=MESH,
            )
            copy.start()
            copies.append(copy)
            waits.append(copy)
        for i, copy in enumerate(copies):
            copy.wait_recv()
        for i in range(len(copies)):
            packed = packed + recv[i]
    norm_out[0] = jnp.sum(jnp.where(lane < half, packed, 0.0))
    norm_out[1] = jnp.sum(jnp.where(lane == half, packed, 0.0))

    for copy in waits:
        copy.wait_send()


def update(
    entries, chunks, step_ref, norm_ref, grad_ref, w_ref, m_ref, v_ref,
    w_out, m_out, v_out, dir_out, drop_out, bufs, sems,
):
    rows, width = grad_ref.shape
    part = rows // chunks
    steps = jnp.full((8, LANES), step_ref[...], jnp.int32)
    scale_m = (1.0 / (1.0 - int_power(0.9, steps)))[0:1, 0:1]
    scale_v = (1.0 / (1.0 - int_power(0.999, steps)))[0:1, 0:1]
    rms = jnp.sqrt(jnp.full((8, LANES), norm_ref[0], jnp.float32) * (1.0 / entries))[0:1, 0:1]
    clip = jnp.minimum(1.0, 0.05 / (rms + 1e-06))
    copies = []
    for k in range(chunks):
        at = slice(k * part, (k + 1) * part)
        scaled = grad_ref[at, :] * clip
        new_m = 0.9 * m_ref[0, 0, at, :] + 0.1 * scaled
        new_v = 0.999 * v_ref[0, 0, at, :] + 0.001 * (scaled * scaled)
        weights = w_ref[0, 0, at, :]
        direction = (new_m * scale_m) / (jnp.sqrt(new_v * scale_v) + 1e-08) + 0.1 * weights
        values = (weights - 0.001 * direction, new_m, new_v, direction)
        for i, (value, out) in enumerate(zip(values, (w_out, m_out, v_out, dir_out))):
            bufs[i, at, :] = value
            copy = pltpu.make_async_copy(bufs.at[i, pl.ds(k * part, part)], out.at[0, 0, pl.ds(k * part, part)], sems.at[k, i])
            copy.start()
            copies.append(copy)
    drop_out[0] = norm_ref[1].astype(jnp.int32)
    for copy in copies:
        copy.wait()


def body(sizes, grad_parts, drop_flags, owner_order, step_count, master, moment_m, moment_v):
    n = sizes["dp"]
    chips = n // 2
    rows, columns = grad_parts.shape[-2:]
    width = master.shape[-1]
    chunks = rows // 8
    part = rows // chunks
    devices = n * sizes["tensor"] * sizes["pipe"]
    stages = [AXES] if devices <= DIRECT else [(axis,) for axis in AXES]
    peers = []
    for axes in stages:
        size = 1
        for axis in axes:
            size *= sizes[axis]
        peers.append(size - 1)
    entries = rows * columns * sizes["tensor"] * sizes["pipe"]
    padded = -(-rows // LANES) * LANES
    others = max(chips - 1, 1)
    f32 = jnp.float32
    dma = pltpu.SemaphoreType.DMA
    vmem = pl.BlockSpec(memory_space=pltpu.VMEM)
    smem = pl.BlockSpec(memory_space=pltpu.SMEM)
    hbm = pl.BlockSpec(memory_space=pltpu.HBM)
    state = jax.ShapeDtypeStruct(master.shape, f32)
    room = rows * columns * 4 - (64 << 10)
    grad, norm = pl.pallas_call(
        functools.partial(kernel, sizes, stages, chunks),
        out_shape=(
            jax.ShapeDtypeStruct((rows, width), f32),
            jax.ShapeDtypeStruct((2,), f32),
        ),
        in_specs=[hbm, hbm, hbm],
        out_specs=(vmem, smem),
        scratch_shapes=[
            pltpu.SMEM((n,), jnp.int32),
            pltpu.VMEM((1, 1, rows), jnp.int32),
            [pltpu.VMEM((part, columns), f32) for _ in range(chunks)],
            pltpu.VMEM((chunks, chips, part, width), f32),
            pltpu.VMEM((chunks, chips, part, width), f32),
            pltpu.VMEM((chunks, others, part, width), f32),
            pltpu.VMEM((chunks, others, part, width), f32),
            pltpu.VMEM((1, 1, padded), f32),
            pltpu.VMEM((n - 1, 1, padded), f32),
            [pltpu.VMEM((1, 1, LANES), f32) for _ in peers],
            [pltpu.VMEM((max(size, 1), 1, LANES), f32) for size in peers],
            dma((2,)),
            dma((chunks,)),
            dma((chunks, chips)),
            dma((chunks, chips)),
            dma((chunks, others)),
            dma((chunks, others)),
            dma((n - 1,)),
            dma((n - 1,)),
            [dma((max(size, 1),)) for size in peers],
            [dma((max(size, 1),)) for size in peers],
        ],
        compiler_params=pltpu.CompilerParams(
            collective_id=0, has_side_effects=True, vmem_limit_bytes=VMEM_MOST - room
        ),
        cost_estimate=pl.CostEstimate(
            flops=8 * rows * columns, bytes_accessed=20 * rows * columns * 4, transcendentals=0
        ),
    )(owner_order, drop_flags.reshape(drop_flags.shape[-3:]), grad_parts)
    outs = pl.pallas_call(
        functools.partial(update, entries, chunks),
        out_shape=(state, state, state, state, jax.ShapeDtypeStruct((1,), jnp.int32)),
        in_specs=[smem, smem, vmem, vmem, vmem, vmem],
        out_specs=(hbm, hbm, hbm, hbm, smem),
        scratch_shapes=[pltpu.VMEM((4, rows, width), f32), dma((chunks, 4))],
        compiler_params=pltpu.CompilerParams(vmem_limit_bytes=VMEM_MOST - 7 * rows * width),
        cost_estimate=pl.CostEstimate(
            flops=20 * rows * width, bytes_accessed=8 * rows * width * 4, transcendentals=0
        ),
    )(step_count, norm, grad, master, moment_m, moment_v)
    return (*outs[:4], outs[4].reshape(()))


def solution(mesh):
    return jax.shard_map(
        functools.partial(body, dict(mesh.shape)),
        mesh=mesh,
        in_specs=(
            P("dp", "pipe", "tensor", None, None),
            P("dp", "pipe", "tensor", None),
            P(),
            P(),
            P("pipe", "tensor", None, "dp"),
            P("pipe", "tensor", None, "dp"),
            P("pipe", "tensor", None, "dp"),
        ),
        out_specs=(
            P("pipe", "tensor", None, "dp"),
            P("pipe", "tensor", None, "dp"),
            P("pipe", "tensor", None, "dp"),
            P("pipe", "tensor", None, "dp"),
            P(),
        ),
        check_vma=False,
    )
```

profile of v0, /device:TPU:0, one launch (start us, length us, event | category | flops | bytes accessed | tf_op | source)
XLA Modules:
  0.0 31.5 jit_solution(247218576956095870)
XLA Ops:
  1.3 26.5 %shard_map.110 = (f32[64,2048]{1,0:T(8,128)}, f32[2]{0:T(128)}) custom-call(s32[4]{0:T(128)} %order_hbm.1, s32[1,1,64]{2,1,0:T(1,128)} %bitcast.2, f32[1,1,1,64,8192]{4,3,2,1,0:T(8,128)} %grad_hbm.1), custom_call_target="tpu_custom_call" | custom-call | flops 4194304 | bytes 41943040 | tf_op jit(solution)/shard_map/pallas_call | solution.py:247
  27.8 3.7 %shard_map.111 = (f32[1,1,64,2048]{3,2,1,0:T(8,128)}, f32[1,1,64,2048]{3,2,1,0:T(8,128)}, f32[1,1,64,2048]{3,2,1,0:T(8,128)}, f32[1,1,64,2048]{3,2,1,0:T(8,128)}, s32[1]{0:T(128)}) custom-call(s32[]{:T(128)S(6)} %copy.12.step_ref, f32[2]{0:T(128)} %get-tuple-element.12.norm_ref, f32[64,2048]{1,0:T(8,128)} %get-tuple-element.13.grad_ref, ...), custom_call_target="tpu_custom_call" | custom-call | flops 2621440 | bytes 4194304 | tf_op jit(solution)/shard_map/pallas_call | solution.py:285
where the time goes:
time: 31.7 us; the launch traced here: 31.5 us
  Pallas kernels  30.2 us (95%)
  between operations  1.29 us (4%)
    pallas_call x1, Pallas kernels, body(): pl.pallas_call(functools.partial(kernel, sizes, stages, chunks), out_shap...  26.5 us
    pallas_call x1, Pallas kernels, body(): pl.pallas_call(functools.partial(update, entries, chunks), out_shape=(sta...  3.73 us

commit v1 on v0

v1 whole, which is shorter than its diff:
```python
import functools
import itertools
import jax
import jax.numpy as jnp
from jax import lax
from jax.experimental import pallas as pl
from jax.experimental.pallas import tpu as pltpu
from jax.sharding import PartitionSpec as P

AXES = ("dp", "tensor", "pipe")
MESH = pl.DeviceIdType.MESH
LANES = 128
SUBLANES = 8
DIRECT = 64


def as_column(row, rows):
    square = (rows, rows)
    diagonal = lax.broadcasted_iota(jnp.int32, square, 0) == lax.broadcasted_iota(jnp.int32, square, 1)
    return jnp.sum(jnp.where(diagonal, jnp.broadcast_to(row, square), 0.0), axis=1, keepdims=True)


def int_power(base, exponent):
    result = jnp.ones(exponent.shape, jnp.float32)
    square = jnp.full(exponent.shape, base, jnp.float32)
    for bit in range(31):
        result = jnp.where((exponent >> bit) & 1 == 1, result * square, result)
        square = square * square
    return result


def exchange(
    sizes, stages, cuts,
    order_hbm, flags_hbm, grad_hbm, w_hbm, m_hbm, v_hbm,
    total, w_vmem, m_vmem, v_vmem, stats,
    order_ref, flags_ref, g_bufs, pair_send, pair_recv, ring_send, ring_recv,
    kept_send, kept_recv, red_sends, red_recvs,
    o_sem, g_sem, w_sem, ps_sem, pr_sem, rs_sem, rr_sem, k_sem, a_sem, ready_sem,
):
    n = sizes["dp"]
    chips = n // 2
    rows, width = total.shape
    parts = [(start, end - start) for start, end in zip(cuts, cuts[1:])]
    me = {axis: lax.axis_index(axis) for axis in AXES}
    chip, core = lax.div(me["dp"], 2), lax.rem(me["dp"], 2)

    def peer(offsets):
        return {axis: lax.rem(me[axis] + off, sizes[axis]) for axis, off in offsets.items()}

    def offsets_of(axes):
        ranges = [range(sizes[axis]) for axis in axes]
        return [dict(zip(axes, offs)) for offs in itertools.product(*ranges) if any(offs)]

    small = [
        pltpu.make_async_copy(flags_hbm, flags_ref, o_sem.at[0]),
        pltpu.make_async_copy(order_hbm, order_ref, o_sem.at[1]),
    ]
    for copy in small:
        copy.start()
    loads = []
    for k, (start, size) in enumerate(parts):
        for b in range(n):
            pltpu.make_async_copy(
                grad_hbm.at[0, 0, 0, pl.ds(start, size), pl.ds(b * width, width)], g_bufs[k].at[b], g_sem.at[k]
            ).start()
        loads.append(pltpu.make_async_copy(g_bufs[k], g_bufs[k], g_sem.at[k]))

    def greet(sem, axis):
        if axis == "dp":
            for off in range(1, n):
                pl.semaphore_signal(sem, inc=1, device_id=peer({"dp": off}), device_id_type=MESH)
            return n - 1
        at, last = me[axis], sizes[axis] - 1

        @pl.when(at > 0)
        def _():
            pl.semaphore_signal(sem, inc=1, device_id={axis: at - 1}, device_id_type=MESH)

        @pl.when(at < last)
        def _():
            pl.semaphore_signal(sem, inc=1, device_id={axis: at + 1}, device_id_type=MESH)

        return jnp.minimum(at, 1) + jnp.minimum(last - at, 1)

    barrier = pltpu.get_barrier_semaphore()
    met = sum(greet(barrier, axis) for axis in AXES)
    rounds = ["pipe"] * max(sizes["pipe"] - 2, 0) + ["tensor"] * (sizes["tensor"] - 1) + ["dp"]
    left, owed = list(rounds), []

    def next_round():
        if owed:
            at, amount = owed.pop()
            pl.semaphore_wait(ready_sem.at[at], amount)
        if left:
            at = len(rounds) - len(left)
            owed.append((at, greet(ready_sem.at[at], left.pop(0))))

    for copy in small:
        copy.wait()
    flags_row = flags_ref[0].astype(jnp.float32)
    kept_row = 1.0 - flags_row
    kept = as_column(kept_row, rows)
    kept_send[0, :, 0:rows] = kept_row
    dropped = jnp.sum(flags_row, axis=1, keepdims=True)

    def chip_at(slot):
        return lax.rem(chip + slot, chips)

    def term(k, owner):
        start, size = parts[k]
        return g_bufs[k][order_ref[owner]] * kept[start:start + size]

    def rows_of(ref, slot, k):
        start, size = parts[k]
        return ref.at[slot, pl.ds(start, size)]

    sibling = {"dp": chip * 2 + 1 - core}
    pair = {}

    def send_pair(k, slot):
        copy = pltpu.make_async_remote_copy(
            rows_of(pair_send, slot, k), rows_of(pair_recv, slot, k),
            ps_sem.at[0], pr_sem.at[k if slot else len(parts)],
            device_id=sibling, device_id_type=MESH,
        )
        copy.start()
        pair[k, slot] = copy

    far = list(range(1, chips))
    for k, (start, size) in enumerate(parts):
        with jax.named_scope(f"load_wait{k}"):
            loads[k].wait()
        for slot in far:
            pair_send[slot, start:start + size, :] = term(k, chip_at(slot) * 2 + 1 - core)
        if k == 0:
            with jax.named_scope("barrier_wait"):
                pl.semaphore_wait(barrier, met)
        for slot in far:
            send_pair(k, slot)
        if k == 0:
            for off in range(1, n):
                pltpu.make_async_remote_copy(
                    kept_send.at[0], kept_recv.at[off - 1], k_sem.at[0], k_sem.at[1],
                    device_id=peer({"dp": off}), device_id_type=MESH,
                ).start()
    kepts = pltpu.make_async_remote_copy(
        kept_recv, kept_recv, k_sem.at[0], k_sem.at[1], device_id=sibling, device_id_type=MESH
    )

    ring = {}
    for k, (start, size) in enumerate(parts):
        for slot in far:
            target = chip_at(slot) * 2 + core
            mine = term(k, target)
            with jax.named_scope(f"pair_wait{k}"):
                if slot == far[0]:
                    pltpu.make_async_remote_copy(
                        pair_recv.at[pl.ds(1, chips - 1), pl.ds(start, size)],
                        pair_recv.at[pl.ds(1, chips - 1), pl.ds(start, size)],
                        ps_sem.at[0], pr_sem.at[k], device_id=sibling, device_id_type=MESH,
                    ).wait_recv()
            ring_send[slot - 1, start:start + size, :] = pair_recv[slot, start:start + size, :] + mine
            copy = pltpu.make_async_remote_copy(
                rows_of(ring_send, slot - 1, k), rows_of(ring_recv, slot - 1, k),
                rs_sem.at[0], rr_sem.at[k, slot - 1],
                device_id={"dp": target}, device_id_type=MESH,
            )
            copy.start()
            ring[k, slot] = copy

    next_round()
    for k, (start, size) in enumerate(parts):
        pair_send[0, start:start + size, :] = term(k, chip * 2 + 1 - core)
        send_pair(k, 0)
    with jax.named_scope("kept_wait"):
        kepts.wait_recv()
    count_row = kept_row
    for i in range(n - 1):
        count_row = count_row + kept_recv[i, :, 0:rows]
    inverse = 1.0 / jnp.maximum(as_column(count_row, rows), 1.0)
    states = []
    for i, (source, target) in enumerate(((w_hbm, w_vmem), (m_hbm, m_vmem), (v_hbm, v_vmem))):
        copy = pltpu.make_async_copy(source.at[0, 0], target, w_sem.at[i])
        copy.start()
        states.append(copy)

    pltpu.make_async_remote_copy(
        pair_recv.at[0], pair_recv.at[0], ps_sem.at[0], pr_sem.at[len(parts)],
        device_id=sibling, device_id_type=MESH,
    ).wait_recv()
    for k, (start, size) in enumerate(parts):
        total[start:start + size, :] = pair_recv[0, start:start + size, :] + term(k, me["dp"])
    for copy in states:
        copy.wait()

    per_part = -(-(len(rounds) + 1) // max(len(parts) - 1, 1))
    squares = jnp.zeros((SUBLANES, LANES), jnp.float32)
    for k, (start, size) in enumerate(parts):
        at = slice(start, start + size)
        value = total[at, :]
        for slot in far:
            with jax.named_scope(f"ring_wait{k}"):
                ring[k, slot].wait_recv()
            value = value + ring_recv[slot - 1, at, :]
        value = value * inverse[at]
        total[at, :] = value
        squares = squares + jnp.sum(
            (value * value).reshape(size // SUBLANES, SUBLANES, width // LANES, LANES), axis=(0, 2)
        )
        for _ in range(per_part):
            next_round()

    result = [jnp.sum(squares, axis=0, keepdims=True), jnp.broadcast_to(dropped, (1, LANES))]
    done = []
    for stage, (axes, send, recv) in enumerate(zip(stages, red_sends, red_recvs)):
        for i, row in enumerate(result):
            send[i:i + 1, :] = row
        with jax.named_scope("norm_send"):
            for i, off in enumerate(offsets_of(axes)):
                pltpu.make_async_remote_copy(
                    send, recv.at[i], a_sem.at[stage, 0], a_sem.at[stage, 1],
                    device_id=peer(off), device_id_type=MESH,
                ).start()
        copy = pltpu.make_async_remote_copy(
            recv, recv, a_sem.at[stage, 0], a_sem.at[stage, 1], device_id=sibling, device_id_type=MESH
        )
        done.append(copy)
        with jax.named_scope("norm_wait"):
            copy.wait_recv()
        for i in range(len(offsets_of(axes))):
            result = [row + recv[i, j:j + 1, :] for j, row in enumerate(result)]
    for i, row in enumerate(result):
        stats[i:i + 1, :] = row
    stats[2:8, :] = jnp.zeros((6, LANES), jnp.float32)

    with jax.named_scope("send_wait"):
        pltpu.make_async_remote_copy(
            pair_send, pair_recv, ps_sem.at[0], pr_sem.at[0], device_id=sibling, device_id_type=MESH
        ).wait_send()
        kepts.wait_send()
        if far:
            pltpu.make_async_remote_copy(
                ring_send, ring_recv, rs_sem.at[0], rr_sem.at[0, 0], device_id=sibling, device_id_type=MESH
            ).wait_send()
        for copy in done:
            copy.wait_send()


def update(
    entries, chunks, step_ref, stats, grad_ref, w_ref, m_ref, v_ref,
    w_out, m_out, v_out, dir_out, drop_out, bufs, drop_ref, sems,
):
    rows, width = grad_ref.shape
    part = rows // chunks
    steps = jnp.full((SUBLANES, LANES), step_ref[...], jnp.int32)
    scale_m = (1.0 / (1.0 - int_power(0.9, steps)))[0:1, 0:1]
    scale_v = (1.0 / (1.0 - int_power(0.999, steps)))[0:1, 0:1]
    summed = jnp.sum(jnp.broadcast_to(stats[0:1, :], (SUBLANES, LANES)), axis=1, keepdims=True)
    rms = jnp.sqrt(summed * (1.0 / entries))[0:1]
    clip = jnp.minimum(1.0, 0.05 / (rms + 1e-06))
    outs = (w_out, m_out, v_out, dir_out)
    for k in range(chunks):
        at = slice(k * part, (k + 1) * part)
        scaled = grad_ref[at, :] * clip
        new_m = 0.9 * m_ref[at, :] + 0.1 * scaled
        new_v = 0.999 * v_ref[at, :] + 0.001 * (scaled * scaled)
        weights = w_ref[at, :]
        direction = (new_m * scale_m) / (jnp.sqrt(new_v * scale_v) + 1e-08) + 0.1 * weights
        values = (weights - 0.001 * direction, new_m, new_v, direction)
        for i, (value, out) in enumerate(zip(values, outs)):
            bufs[i, at, :] = value
            pltpu.make_async_copy(bufs.at[i, pl.ds(k * part, part)], out.at[0, 0, pl.ds(k * part, part)], sems.at[i]).start()
        if k == 0:
            drop_ref[0] = jnp.max(stats[1:2, :]).astype(jnp.int32)
            drop = pltpu.make_async_copy(drop_ref, drop_out, sems.at[4])
            drop.start()
    for i, out in enumerate(outs):
        pltpu.make_async_copy(bufs.at[i], out.at[0, 0], sems.at[i]).wait()
    drop.wait()


def body(sizes, grad_parts, drop_flags, owner_order, step_count, master, moment_m, moment_v):
    n = sizes["dp"]
    chips = n // 2
    rows, columns = grad_parts.shape[-2:]
    width = master.shape[-1]
    chunks = rows // 8
    cuts = sorted({0, 8, rows // 2, rows - 8, rows})
    devices = n * sizes["tensor"] * sizes["pipe"]
    stages = [AXES] if devices <= DIRECT else [(axis,) for axis in AXES]
    peers = []
    for axes in stages:
        size = 1
        for axis in axes:
            size *= sizes[axis]
        peers.append(size - 1)
    entries = rows * columns * sizes["tensor"] * sizes["pipe"]
    padded = -(-rows // LANES) * LANES
    others = max(chips - 1, 1)
    rounds = max(sizes["pipe"] - 2, 0) + sizes["tensor"]
    f32 = jnp.float32
    dma = pltpu.SemaphoreType.DMA
    vmem = pl.BlockSpec(memory_space=pltpu.VMEM)
    smem = pl.BlockSpec(memory_space=pltpu.SMEM)
    hbm = pl.BlockSpec(memory_space=pltpu.HBM)
    state = jax.ShapeDtypeStruct(master.shape, f32)
    held = pltpu.VMEM((rows, width), f32)
    block = rows * columns * 4
    inputs = (owner_order, drop_flags.reshape(drop_flags.shape[-3:]), grad_parts, master, moment_m, moment_v)
    total, weights, first, second, stats = pl.pallas_call(
        functools.partial(exchange, sizes, stages, cuts),
        out_shape=(held, held, held, held, pltpu.VMEM((SUBLANES, LANES), f32)),
        in_specs=[hbm] * 6,
        out_specs=(vmem,) * 5,
        scratch_shapes=[
            pltpu.SMEM((n,), jnp.int32),
            pltpu.VMEM((1, 1, rows), jnp.int32),
            [pltpu.VMEM((n, end - start, width), f32) for start, end in zip(cuts, cuts[1:])],
            pltpu.VMEM((chips, rows, width), f32),
            pltpu.VMEM((chips, rows, width), f32),
            pltpu.VMEM((others, rows, width), f32),
            pltpu.VMEM((others, rows, width), f32),
            pltpu.VMEM((1, 1, padded), f32),
            pltpu.VMEM((n - 1, 1, padded), f32),
            [pltpu.VMEM((2, LANES), f32) for _ in peers],
            [pltpu.VMEM((max(size, 1), 2, LANES), f32) for size in peers],
            dma((2,)),
            dma((len(cuts) - 1,)),
            dma((3,)),
            dma((1,)),
            dma((len(cuts),)),
            dma((1,)),
            dma((len(cuts) - 1, others)),
            dma((2,)),
            dma((len(peers), 2)),
            pltpu.SemaphoreType.REGULAR((rounds,)),
        ],
        compiler_params=pltpu.CompilerParams(
            collective_id=0, has_side_effects=True, vmem_limit_bytes=8 * block
        ),
        cost_estimate=pl.CostEstimate(
            flops=8 * rows * columns, bytes_accessed=20 * rows * columns * 4, transcendentals=0
        ),
    )(*(pltpu.with_memory_space_constraint(x, pltpu.HBM) for x in inputs))
    outs = pl.pallas_call(
        functools.partial(update, entries, chunks),
        out_shape=(state, state, state, state, jax.ShapeDtypeStruct((1,), jnp.int32)),
        in_specs=[smem] + [vmem] * 5,
        out_specs=(hbm,) * 5,
        scratch_shapes=[pltpu.VMEM((4, rows, width), f32), pltpu.SMEM((1,), jnp.int32), dma((5,))],
        compiler_params=pltpu.CompilerParams(vmem_limit_bytes=8 * block),
        cost_estimate=pl.CostEstimate(
            flops=20 * rows * width, bytes_accessed=8 * rows * width * 4, transcendentals=0
        ),
    )(step_count, stats, total, weights, first, second)
    return (*outs[:4], outs[4].reshape(()))


def solution(mesh):
    return jax.shard_map(
        functools.partial(body, dict(mesh.shape)),
        mesh=mesh,
        in_specs=(
            P("dp", "pipe", "tensor", None, None),
            P("dp", "pipe", "tensor", None),
            P(),
            P(),
            P("pipe", "tensor", None, "dp"),
            P("pipe", "tensor", None, "dp"),
            P("pipe", "tensor", None, "dp"),
        ),
        out_specs=(
            P("pipe", "tensor", None, "dp"),
            P("pipe", "tensor", None, "dp"),
            P("pipe", "tensor", None, "dp"),
            P("pipe", "tensor", None, "dp"),
            P(),
        ),
        check_vma=False,
    )
```

time: 31.7 us -> 27.4 us (0.86)
  Pallas kernels: 30.2 us -> 25.9 us
    pallas_call x1, Pallas kernels: 3.73 us -> 1.49 us  [body(): pl.pallas_call(functools.partial(update, entries, chunks), out_shape=(sta...]
    pallas_call x1, Pallas kernels: 26.5 us -> 24.4 us  [body(): pl.pallas_call(functools.partial(exchange, sizes, stages, cuts), out_shap...]
where the time goes in v1:
time: 27.4 us; the launch traced here: 27.2 us
  Pallas kernels  25.9 us (95%)
  between operations  1.29 us (5%)
    pallas_call x1, Pallas kernels, body(): pl.pallas_call(functools.partial(exchange, sizes, stages, cuts), out_shap...  24.4 us
    pallas_call x1, Pallas kernels, body(): pl.pallas_call(functools.partial(update, entries, chunks), out_shape=(sta...  1.49 us

profile of v1, /device:TPU:0, one launch (start us, length us, event | category | flops | bytes accessed | tf_op | source)
XLA Modules:
  0.0 27.2 jit_solution(17729672378831606765)
XLA Ops:
  1.3 24.4 %shard_map.110 = (f32[64,2048]{1,0:T(8,128)S(1)}, f32[64,2048]{1,0:T(8,128)S(1)}, f32[64,2048]{1,0:T(8,128)S(1)}, f32[64,2048]{1,0:T(8,128)S(1)}, f32[8,128]{1,0:T(8,128)S(1)}) custom-call(s32[4]{0:T(128)} %order_hbm.1, s32[1,1,64]{2,1,0:T(1,128)} %bitcast.2, f32[1,1,1,64,8192]{4,3,2,1,0:T(8,128)} %grad_hbm.1, f32[1,1,64,2048]{3,2,1,0:T(8,128)} %w_hbm.1, ...), custom_call_target="tpu_custom_call" | custom-call | flops 4194304 | bytes 41943040 | tf_op jit(solution)/shard_map/pallas_call | solution.py:310
  25.7 1.5 %shard_map.111 = (f32[1,1,64,2048]{3,2,1,0:T(8,128)}, f32[1,1,64,2048]{3,2,1,0:T(8,128)}, f32[1,1,64,2048]{3,2,1,0:T(8,128)}, f32[1,1,64,2048]{3,2,1,0:T(8,128)}, s32[1]{0:T(128)}) custom-call(s32[]{:T(128)S(6)} %copy.12.step_ref, f32[8,128]{1,0:T(8,128)S(1)} %get-tuple-element.15.stats, f32[64,2048]{1,0:T(8,128)S(1)} %get-tuple-element.16.grad_ref, ...), custom_call_target="tpu_custom_call" | custom-call | flops 2621440 | bytes 4194304 | tf_op jit(solution)/shard_map/pallas_call | solution.py:345

commit v2 on v1

--- a/solution.py
+++ b/solution.py
@@ -1,5 +1,6 @@
 import functools
 import itertools
+import math
 import jax
 import jax.numpy as jnp
 from jax import lax
@@ -12,6 +13,7 @@
 LANES = 128
 SUBLANES = 8
 DIRECT = 64
+PIECES = 4
 
 
 def as_column(row, rows):
@@ -29,16 +31,21 @@
     return result
 
 
+def can_relay(sizes, stages):
+    return sizes["dp"] == 4 and sizes["tensor"] == 2 and len(stages) == 1 and sizes["pipe"] > 1
+
+
 def exchange(
     sizes, stages, cuts,
-    order_hbm, flags_hbm, grad_hbm, w_hbm, m_hbm, v_hbm,
-    total, w_vmem, m_vmem, v_vmem, stats,
+    step_ref, order_hbm, flags_hbm, grad_hbm, w_hbm, m_hbm, v_hbm,
+    total, held, stats,
     order_ref, flags_ref, g_bufs, pair_send, pair_recv, ring_send, ring_recv,
     kept_send, kept_recv, red_sends, red_recvs,
-    o_sem, g_sem, w_sem, ps_sem, pr_sem, rs_sem, rr_sem, k_sem, a_sem, ready_sem,
+    relay_buf, o_sem, g_sem, w_sem, ps_sem, pr_sem, rs_sem, rr_sem, k_sem, a_sem, via_sem, chain_sem, ready_sem,
 ):
     n = sizes["dp"]
     chips = n // 2
+    relayed = can_relay(sizes, stages)
     rows, width = total.shape
     parts = [(start, end - start) for start, end in zip(cuts, cuts[1:])]
     me = {axis: lax.axis_index(axis) for axis in AXES}
@@ -58,12 +65,16 @@
     for copy in small:
         copy.start()
     loads = []
-    for k, (start, size) in enumerate(parts):
+
+    def load(k):
+        start, size = parts[k]
         for b in range(n):
             pltpu.make_async_copy(
                 grad_hbm.at[0, 0, 0, pl.ds(start, size), pl.ds(b * width, width)], g_bufs[k].at[b], g_sem.at[k]
             ).start()
         loads.append(pltpu.make_async_copy(g_bufs[k], g_bufs[k], g_sem.at[k]))
+
+    load(0)
 
     def greet(sem, axis):
         if axis == "dp":
@@ -74,16 +85,28 @@
 
         @pl.when(at > 0)
         def _():
-            pl.semaphore_signal(sem, inc=1, device_id={axis: at - 1}, device_id_type=MESH)
+            pl.semaphore_signal(sem, inc=1, device_id={**home, axis: at - 1}, device_id_type=MESH)
 
         @pl.when(at < last)
         def _():
-            pl.semaphore_signal(sem, inc=1, device_id={axis: at + 1}, device_id_type=MESH)
+            pl.semaphore_signal(sem, inc=1, device_id={**home, axis: at + 1}, device_id_type=MESH)
 
         return jnp.minimum(at, 1) + jnp.minimum(last - at, 1)
 
+    sibling = {"dp": chip * 2 + 1 - core}
     barrier = pltpu.get_barrier_semaphore()
-    met = sum(greet(barrier, axis) for axis in AXES)
+
+    @pl.when(core == 1)
+    def _():
+        pl.semaphore_signal(barrier, inc=1, device_id=sibling, device_id_type=MESH)
+
+    home = {"dp": chip * 2 + 1}
+    for off in range(1, chips):
+        pl.semaphore_signal(
+            barrier, inc=1, device_id={"dp": lax.rem(chip + off, chips) * 2 + 1}, device_id_type=MESH
+        )
+    met = 2 * (chips - 1 + greet(barrier, "tensor") + greet(barrier, "pipe"))
+    home = {}
     rounds = ["pipe"] * max(sizes["pipe"] - 2, 0) + ["tensor"] * (sizes["tensor"] - 1) + ["dp"]
     left, owed = list(rounds), []
 
@@ -95,8 +118,17 @@
             at = len(rounds) - len(left)
             owed.append((at, greet(ready_sem.at[at], left.pop(0))))
 
+    load(1)
+
+    @pl.when(core == 0)
+    def _():
+        pl.semaphore_wait(barrier, 1)
+        pl.semaphore_signal(chain_sem.at[2], inc=1, device_id=sibling, device_id_type=MESH)
+
     for copy in small:
         copy.wait()
+    for k in range(2, len(parts)):
+        load(k)
     flags_row = flags_ref[0].astype(jnp.float32)
     kept_row = 1.0 - flags_row
     kept = as_column(kept_row, rows)
@@ -114,7 +146,6 @@
         start, size = parts[k]
         return ref.at[slot, pl.ds(start, size)]
 
-    sibling = {"dp": chip * 2 + 1 - core}
     pair = {}
 
     def send_pair(k, slot):
@@ -127,28 +158,74 @@
         pair[k, slot] = copy
 
     far = list(range(1, chips))
-    for k, (start, size) in enumerate(parts):
+    def to_sibling(k):
+        start, size = parts[k]
         with jax.named_scope(f"load_wait{k}"):
             loads[k].wait()
         for slot in far:
             pair_send[slot, start:start + size, :] = term(k, chip_at(slot) * 2 + 1 - core)
         if k == 0:
-            with jax.named_scope("barrier_wait"):
-                pl.semaphore_wait(barrier, met)
+            with jax.named_scope("sibling_wait"):
+                @pl.when(core == 1)
+                def _():
+                    pl.semaphore_wait(chain_sem.at[2], 1)
         for slot in far:
             send_pair(k, slot)
-        if k == 0:
-            for off in range(1, n):
-                pltpu.make_async_remote_copy(
-                    kept_send.at[0], kept_recv.at[off - 1], k_sem.at[0], k_sem.at[1],
-                    device_id=peer({"dp": off}), device_id_type=MESH,
-                ).start()
+
     kepts = pltpu.make_async_remote_copy(
         kept_recv, kept_recv, k_sem.at[0], k_sem.at[1], device_id=sibling, device_id_type=MESH
     )
 
     ring = {}
-    for k, (start, size) in enumerate(parts):
+    swing = len(parts) - 2
+    far_end = sizes["pipe"] - 1
+    gap = 2 * me["pipe"] - far_end
+    across = {"dp": chip_at(1) * 2 + core}
+    direct = [k for k in range(len(parts)) if k != swing]
+    lend = [gap >= 1, gap >= 3, 2 * me["tensor"] >= sizes["tensor"]] if relayed else []
+    borrow = [gap <= -1, gap <= -3, 2 * me["tensor"] < sizes["tensor"]] if relayed else []
+    mirror = [{"pipe": far_end - me["pipe"]}] * 2 + [{"tensor": sizes["tensor"] - 1 - me["tensor"]}]
+    quarter = width // PIECES
+
+    def piece(ref, h):
+        start, size = parts[swing]
+        return ref.at[0, pl.ds(start, size), pl.ds(h * quarter, quarter)]
+
+    def swing_copy(h):
+        return pltpu.make_async_remote_copy(
+            piece(ring_send, h), piece(ring_recv, h), rs_sem.at[0], rr_sem.at[swing, 0],
+            device_id=across, device_id_type=MESH,
+        )
+
+    def via_copy(h):
+        return pltpu.make_async_remote_copy(
+            piece(ring_send, h), relay_buf.at[h], rs_sem.at[0], via_sem.at[h],
+            device_id={**across, **mirror[h]}, device_id_type=MESH,
+        )
+
+    def forward_copy(h):
+        return pltpu.make_async_remote_copy(
+            relay_buf.at[h], piece(ring_recv, h), via_sem.at[h], rr_sem.at[swing, 0],
+            device_id=mirror[h], device_id_type=MESH,
+        )
+
+    def climb():
+        at = me["pipe"]
+
+        @pl.when(at >= 2)
+        def _():
+            pl.semaphore_wait(chain_sem.at[0], 1)
+
+        @pl.when((at >= 1) & (at < far_end))
+        def _():
+            pl.semaphore_signal(chain_sem.at[0], inc=1, device_id={"pipe": at + 1}, device_id_type=MESH)
+
+        @pl.when(lend[0] | lend[2])
+        def _():
+            pl.semaphore_signal(chain_sem.at[1], inc=1, device_id=across, device_id_type=MESH)
+
+    def to_owner(k):
+        start, size = parts[k]
         for slot in far:
             target = chip_at(slot) * 2 + core
             mine = term(k, target)
@@ -160,6 +237,24 @@
                         ps_sem.at[0], pr_sem.at[k], device_id=sibling, device_id_type=MESH,
                     ).wait_recv()
             ring_send[slot - 1, start:start + size, :] = pair_recv[slot, start:start + size, :] + mine
+            if relayed and k == swing:
+                @pl.when(lend[0] | lend[2])
+                def _():
+                    with jax.named_scope("chain_wait"):
+                        pl.semaphore_wait(chain_sem.at[1], 1)
+
+                for h, away in enumerate(lend):
+                    @pl.when(away)
+                    def _():
+                        via_copy(h).start()
+
+                for h, away in enumerate(lend):
+                    @pl.when(jnp.logical_not(away))
+                    def _():
+                        swing_copy(h).start()
+                for h in range(len(lend), PIECES):
+                    swing_copy(h).start()
+                continue
             copy = pltpu.make_async_remote_copy(
                 rows_of(ring_send, slot - 1, k), rows_of(ring_recv, slot - 1, k),
                 rs_sem.at[0], rr_sem.at[k, slot - 1],
@@ -167,6 +262,31 @@
             )
             copy.start()
             ring[k, slot] = copy
+
+    to_sibling(0)
+    to_sibling(1)
+    with jax.named_scope("barrier_wait"):
+        @pl.when(core == 1)
+        def _():
+            pl.semaphore_wait(barrier, met)
+            pl.semaphore_signal(chain_sem.at[2], inc=1, device_id=sibling, device_id_type=MESH)
+
+        @pl.when(core == 0)
+        def _():
+            pl.semaphore_wait(chain_sem.at[2], 1)
+    for off in range(1, n):
+        pltpu.make_async_remote_copy(
+            kept_send.at[0], kept_recv.at[off - 1], k_sem.at[0], k_sem.at[1],
+            device_id=peer({"dp": off}), device_id_type=MESH,
+        ).start()
+    to_owner(0)
+    if relayed:
+        climb()
+    to_owner(1)
+    for k in range(2, len(parts)):
+        to_sibling(k)
+    for k in direct[2:] + [swing]:
+        to_owner(k)
 
     next_round()
     for k, (start, size) in enumerate(parts):
@@ -178,11 +298,8 @@
     for i in range(n - 1):
         count_row = count_row + kept_recv[i, :, 0:rows]
     inverse = 1.0 / jnp.maximum(as_column(count_row, rows), 1.0)
-    states = []
-    for i, (source, target) in enumerate(((w_hbm, w_vmem), (m_hbm, m_vmem), (v_hbm, v_vmem))):
-        copy = pltpu.make_async_copy(source.at[0, 0], target, w_sem.at[i])
-        copy.start()
-        states.append(copy)
+    for i, source in enumerate((w_hbm, m_hbm, v_hbm)):
+        pltpu.make_async_copy(source.at[0, 0], held.at[i], w_sem.at[0]).start()
 
     pltpu.make_async_remote_copy(
         pair_recv.at[0], pair_recv.at[0], ps_sem.at[0], pr_sem.at[len(parts)],
@@ -190,8 +307,21 @@
     ).wait_recv()
     for k, (start, size) in enumerate(parts):
         total[start:start + size, :] = pair_recv[0, start:start + size, :] + term(k, me["dp"])
-    for copy in states:
-        copy.wait()
+    pltpu.make_async_copy(held, held, w_sem.at[0]).wait()
+    held[1] = 0.9 * held[1]
+    held[2] = 0.999 * held[2]
+    steps = jnp.full((SUBLANES, LANES), step_ref[...], jnp.int32)
+    stats[0:8, :] = jnp.zeros((SUBLANES, LANES), jnp.float32)
+    stats[8:16, :] = 1.0 / (1.0 - int_power(0.9, steps))
+    stats[16:24, :] = 1.0 / (1.0 - int_power(0.999, steps))
+
+    if relayed:
+        for h in (2, 0, 1):
+            @pl.when(borrow[h])
+            def _():
+                with jax.named_scope(f"relay_wait{h}"):
+                    via_copy(h).wait_recv()
+                forward_copy(h).start()
 
     per_part = -(-(len(rounds) + 1) // max(len(parts) - 1, 1))
     squares = jnp.zeros((SUBLANES, LANES), jnp.float32)
@@ -200,7 +330,13 @@
         value = total[at, :]
         for slot in far:
             with jax.named_scope(f"ring_wait{k}"):
-                ring[k, slot].wait_recv()
+                if relayed and k == swing:
+                    pltpu.make_async_remote_copy(
+                        ring_recv.at[0, pl.ds(start, size)], ring_recv.at[0, pl.ds(start, size)],
+                        rs_sem.at[0], rr_sem.at[swing, 0], device_id=across, device_id_type=MESH,
+                    ).wait_recv()
+                else:
+                    ring[k, slot].wait_recv()
             value = value + ring_recv[slot - 1, at, :]
         value = value * inverse[at]
         total[at, :] = value
@@ -216,11 +352,24 @@
         for i, row in enumerate(result):
             send[i:i + 1, :] = row
         with jax.named_scope("norm_send"):
-            for i, off in enumerate(offsets_of(axes)):
+            back, stride = 0, 1
+            for axis in reversed(axes):
+                back, stride = back + lax.rem(sizes[axis] - me[axis], sizes[axis]) * stride, stride * sizes[axis]
+
+            def share(i, device):
                 pltpu.make_async_remote_copy(
                     send, recv.at[i], a_sem.at[stage, 0], a_sem.at[stage, 1],
-                    device_id=peer(off), device_id_type=MESH,
+                    device_id=device, device_id_type=MESH,
                 ).start()
+
+            @pl.when(back > 0)
+            def _():
+                share(back - 1, dict.fromkeys(axes, 0))
+
+            for i, off in enumerate(offsets_of(axes)):
+                @pl.when(back != i + 1)
+                def _():
+                    share(i, peer(off))
         copy = pltpu.make_async_remote_copy(
             recv, recv, a_sem.at[stage, 0], a_sem.at[stage, 1], device_id=sibling, device_id_type=MESH
         )
@@ -231,7 +380,6 @@
             result = [row + recv[i, j:j + 1, :] for j, row in enumerate(result)]
     for i, row in enumerate(result):
         stats[i:i + 1, :] = row
-    stats[2:8, :] = jnp.zeros((6, LANES), jnp.float32)
 
     with jax.named_scope("send_wait"):
         pltpu.make_async_remote_copy(
@@ -244,28 +392,35 @@
             ).wait_send()
         for copy in done:
             copy.wait_send()
+        if relayed:
+            for h, taken in enumerate(borrow):
+                @pl.when(taken)
+                def _():
+                    forward_copy(h).wait_send()
 
 
 def update(
-    entries, chunks, step_ref, stats, grad_ref, w_ref, m_ref, v_ref,
+    entries, chunks, stats, grad_ref, held,
     w_out, m_out, v_out, dir_out, drop_out, bufs, drop_ref, sems,
 ):
     rows, width = grad_ref.shape
     part = rows // chunks
-    steps = jnp.full((SUBLANES, LANES), step_ref[...], jnp.int32)
-    scale_m = (1.0 / (1.0 - int_power(0.9, steps)))[0:1, 0:1]
-    scale_v = (1.0 / (1.0 - int_power(0.999, steps)))[0:1, 0:1]
+    scale_m = jnp.concatenate([stats[8:16, :]] * (width // LANES), axis=1)
+    scale_v = jnp.concatenate([stats[16:24, :]] * (width // LANES), axis=1)
     summed = jnp.sum(jnp.broadcast_to(stats[0:1, :], (SUBLANES, LANES)), axis=1, keepdims=True)
-    rms = jnp.sqrt(summed * (1.0 / entries))[0:1]
+    rms = jnp.sqrt(summed * (1.0 / entries))
     clip = jnp.minimum(1.0, 0.05 / (rms + 1e-06))
+    share_m, share_v = 0.1 * clip, math.sqrt(0.001) * clip
     outs = (w_out, m_out, v_out, dir_out)
     for k in range(chunks):
         at = slice(k * part, (k + 1) * part)
-        scaled = grad_ref[at, :] * clip
-        new_m = 0.9 * m_ref[at, :] + 0.1 * scaled
-        new_v = 0.999 * v_ref[at, :] + 0.001 * (scaled * scaled)
-        weights = w_ref[at, :]
-        direction = (new_m * scale_m) / (jnp.sqrt(new_v * scale_v) + 1e-08) + 0.1 * weights
+        grad = grad_ref[at, :]
+        root = grad * share_v
+        new_m = held[1, at, :] + grad * share_m
+        new_v = held[2, at, :] + root * root
+        weights = held[0, at, :]
+        corrected = new_v * scale_v
+        direction = (new_m * scale_m) / (corrected * lax.rsqrt(corrected) + 1e-08) + 0.1 * weights
         values = (weights - 0.001 * direction, new_m, new_v, direction)
         for i, (value, out) in enumerate(zip(values, outs)):
             bufs[i, at, :] = value
@@ -285,7 +440,7 @@
     rows, columns = grad_parts.shape[-2:]
     width = master.shape[-1]
     chunks = rows // 8
-    cuts = sorted({0, 8, rows // 2, rows - 8, rows})
+    cuts = sorted({0, 8, rows - 24, rows - 8, rows})
     devices = n * sizes["tensor"] * sizes["pipe"]
     stages = [AXES] if devices <= DIRECT else [(axis,) for axis in AXES]
     peers = []
@@ -304,14 +459,13 @@
     smem = pl.BlockSpec(memory_space=pltpu.SMEM)
     hbm = pl.BlockSpec(memory_space=pltpu.HBM)
     state = jax.ShapeDtypeStruct(master.shape, f32)
-    held = pltpu.VMEM((rows, width), f32)
     block = rows * columns * 4
     inputs = (owner_order, drop_flags.reshape(drop_flags.shape[-3:]), grad_parts, master, moment_m, moment_v)
-    total, weights, first, second, stats = pl.pallas_call(
+    total, held, stats = pl.pallas_call(
         functools.partial(exchange, sizes, stages, cuts),
-        out_shape=(held, held, held, held, pltpu.VMEM((SUBLANES, LANES), f32)),
-        in_specs=[hbm] * 6,
-        out_specs=(vmem,) * 5,
+        out_shape=tuple(pltpu.VMEM(shape, f32) for shape in ((rows, width), (3, rows, width), (3 * SUBLANES, LANES))),
+        in_specs=[smem] + [hbm] * 6,
+        out_specs=(vmem,) * 3,
         scratch_shapes=[
             pltpu.SMEM((n,), jnp.int32),
             pltpu.VMEM((1, 1, rows), jnp.int32),
@@ -324,15 +478,18 @@
             pltpu.VMEM((n - 1, 1, padded), f32),
             [pltpu.VMEM((2, LANES), f32) for _ in peers],
             [pltpu.VMEM((max(size, 1), 2, LANES), f32) for size in peers],
+            pltpu.VMEM((PIECES - 1, 16, width // PIECES), f32),
             dma((2,)),
             dma((len(cuts) - 1,)),
-            dma((3,)),
+            dma((1,)),
             dma((1,)),
             dma((len(cuts),)),
             dma((1,)),
             dma((len(cuts) - 1, others)),
             dma((2,)),
             dma((len(peers), 2)),
+            dma((PIECES - 1,)),
+            pltpu.SemaphoreType.REGULAR((3,)),
             pltpu.SemaphoreType.REGULAR((rounds,)),
         ],
         compiler_params=pltpu.CompilerParams(
@@ -341,18 +498,18 @@
         cost_estimate=pl.CostEstimate(
             flops=8 * rows * columns, bytes_accessed=20 * rows * columns * 4, transcendentals=0
         ),
-    )(*(pltpu.with_memory_space_constraint(x, pltpu.HBM) for x in inputs))
+    )(step_count, *(pltpu.with_memory_space_constraint(x, pltpu.HBM) for x in inputs))
     outs = pl.pallas_call(
         functools.partial(update, entries, chunks),
         out_shape=(state, state, state, state, jax.ShapeDtypeStruct((1,), jnp.int32)),
-        in_specs=[smem] + [vmem] * 5,
+        in_specs=[vmem] * 3,
         out_specs=(hbm,) * 5,
         scratch_shapes=[pltpu.VMEM((4, rows, width), f32), pltpu.SMEM((1,), jnp.int32), dma((5,))],
         compiler_params=pltpu.CompilerParams(vmem_limit_bytes=8 * block),
         cost_estimate=pl.CostEstimate(
             flops=20 * rows * width, bytes_accessed=8 * rows * width * 4, transcendentals=0
         ),
-    )(step_count, stats, total, weights, first, second)
+    )(stats, total, held)
     return (*outs[:4], outs[4].reshape(()))
 
 

time: 27.4 us -> 25.2 us (0.920)
  Pallas kernels: 25.9 us -> 23.8 us
    pallas_call x1, Pallas kernels: 24.4 us -> 22.3 us  [body(): pl.pallas_call(functools.partial(exchange, sizes, stages, cuts), out_shap...]
where the time goes in v2:
time: 25.2 us; the launch traced here: 25 us
  Pallas kernels  23.8 us (94%)
  between operations  1.29 us (5%)
    pallas_call x1, Pallas kernels, body(): pl.pallas_call(functools.partial(exchange, sizes, stages, cuts), out_shap...  22.3 us
    pallas_call x1, Pallas kernels, body(): pl.pallas_call(functools.partial(update, entries, chunks), out_shape=(sta...  1.48 us

profile of v2, /device:TPU:0, one launch (start us, length us, event | category | flops | bytes accessed | tf_op | source)
XLA Modules:
  0.0 25.0 jit_solution(15443989141790892137)
XLA Ops:
  1.3 22.3 %shard_map.110 = (f32[64,2048]{1,0:T(8,128)S(1)}, f32[3,64,2048]{2,1,0:T(8,128)S(1)}, f32[24,128]{1,0:T(8,128)S(1)}) custom-call(s32[]{:T(128)S(6)} %copy.12.step_ref, s32[4]{0:T(128)} %order_hbm.1, s32[1,1,64]{2,1,0:T(1,128)} %bitcast.2, f32[1,1,1,64,8192]{4,3,2,1,0:T(8,128)} %grad_hbm.1, f32[1,1,64,2048]{3,2,1,0:T(8,128)} %w_hbm.1, ...), custom_call_target="tpu_custom_call" | custom-call | flops 4194304 | bytes 41943040 | tf_op jit(solution)/shard_map/pallas_call | solution.py:464
  23.6 1.5 %shard_map.111 = (f32[1,1,64,2048]{3,2,1,0:T(8,128)}, f32[1,1,64,2048]{3,2,1,0:T(8,128)}, f32[1,1,64,2048]{3,2,1,0:T(8,128)}, f32[1,1,64,2048]{3,2,1,0:T(8,128)}, s32[1]{0:T(128)}) custom-call(f32[24,128]{1,0:T(8,128)S(1)} %get-tuple-element.13.stats, f32[64,2048]{1,0:T(8,128)S(1)} %get-tuple-element.14.grad_ref, f32[3,64,2048]{2,1,0:T(8,128)S(1)} %get-tuple-element.15.held), custom_call_target="tpu_custom_call" | custom-call | flops 2621440 | bytes 4194304 | tf_op jit(solution)/shard_map/pallas_call | solution.py:502

commit v3 on v2

--- a/solution.py
+++ b/solution.py
@@ -13,7 +13,8 @@
 LANES = 128
 SUBLANES = 8
 DIRECT = 64
-PIECES = 4
+EDGES = (0, 3, 8, 11, 16)
+PIECES = len(EDGES) - 1
 
 
 def as_column(row, rows):
@@ -41,7 +42,7 @@
     total, held, stats,
     order_ref, flags_ref, g_bufs, pair_send, pair_recv, ring_send, ring_recv,
     kept_send, kept_recv, red_sends, red_recvs,
-    relay_buf, o_sem, g_sem, w_sem, ps_sem, pr_sem, rs_sem, rr_sem, k_sem, a_sem, via_sem, chain_sem, ready_sem,
+    relay_buf, tail_send, tail_recv, tail_ring, o_sem, g_sem, w_sem, ps_sem, pr_sem, rs_sem, rr_sem, k_sem, a_sem, via_sem, tail_sem, chain_sem, ready_sem,
 ):
     n = sizes["dp"]
     chips = n // 2
@@ -151,7 +152,7 @@
     def send_pair(k, slot):
         copy = pltpu.make_async_remote_copy(
             rows_of(pair_send, slot, k), rows_of(pair_recv, slot, k),
-            ps_sem.at[0], pr_sem.at[k if slot else len(parts)],
+            ps_sem.at[1 if slot else 0], pr_sem.at[k if slot else len(parts)],
             device_id=sibling, device_id_type=MESH,
         )
         copy.start()
@@ -181,15 +182,17 @@
     far_end = sizes["pipe"] - 1
     gap = 2 * me["pipe"] - far_end
     across = {"dp": chip_at(1) * 2 + core}
-    direct = [k for k in range(len(parts)) if k != swing]
     lend = [gap >= 1, gap >= 3, 2 * me["tensor"] >= sizes["tensor"]] if relayed else []
     borrow = [gap <= -1, gap <= -3, 2 * me["tensor"] < sizes["tensor"]] if relayed else []
     mirror = [{"pipe": far_end - me["pipe"]}] * 2 + [{"tensor": sizes["tensor"] - 1 - me["tensor"]}]
-    quarter = width // PIECES
+    edges = [width * edge // 16 for edge in EDGES]
 
     def piece(ref, h):
         start, size = parts[swing]
-        return ref.at[0, pl.ds(start, size), pl.ds(h * quarter, quarter)]
+        return ref.at[0, pl.ds(start, size), pl.ds(edges[h], edges[h + 1] - edges[h])]
+
+    def lodging(h):
+        return relay_buf.at[h, :, pl.ds(0, edges[h + 1] - edges[h])]
 
     def swing_copy(h):
         return pltpu.make_async_remote_copy(
@@ -199,13 +202,13 @@
 
     def via_copy(h):
         return pltpu.make_async_remote_copy(
-            piece(ring_send, h), relay_buf.at[h], rs_sem.at[0], via_sem.at[h],
+            piece(ring_send, h), lodging(h), rs_sem.at[0], via_sem.at[h],
             device_id={**across, **mirror[h]}, device_id_type=MESH,
         )
 
     def forward_copy(h):
         return pltpu.make_async_remote_copy(
-            relay_buf.at[h], piece(ring_recv, h), via_sem.at[h], rr_sem.at[swing, 0],
+            lodging(h), piece(ring_recv, h), via_sem.at[h], rr_sem.at[swing, 0],
             device_id=mirror[h], device_id_type=MESH,
         )
 
@@ -223,6 +226,38 @@
         @pl.when(lend[0] | lend[2])
         def _():
             pl.semaphore_signal(chain_sem.at[1], inc=1, device_id=across, device_id_type=MESH)
+
+    tail = len(parts) - 1
+    tail_at = pl.ds(*parts[tail])
+    abroad = chip_at(1) * 2
+
+    def tail_pair():
+        return pltpu.make_async_remote_copy(
+            tail_send, tail_recv, tail_sem.at[0], tail_sem.at[0], device_id=sibling, device_id_type=MESH
+        )
+
+    def tail_copy(c):
+        return pltpu.make_async_remote_copy(
+            tail_ring.at[c], ring_recv.at[0, tail_at], tail_sem.at[1], rr_sem.at[tail, 0],
+            device_id={"dp": abroad + c}, device_id_type=MESH,
+        )
+
+    def tail_to_sibling():
+        loads[tail].wait()
+
+        @pl.when(core == 0)
+        def _():
+            for c in range(2):
+                tail_send[c] = term(tail, abroad + c)
+            tail_pair().start()
+
+    def tail_to_owner():
+        @pl.when(core == 1)
+        def _():
+            tail_pair().wait_recv()
+            for c in range(2):
+                tail_ring[c] = tail_recv[c] + term(tail, abroad + c)
+                tail_copy(c).start()
 
     def to_owner(k):
         start, size = parts[k]
@@ -282,11 +317,19 @@
     to_owner(0)
     if relayed:
         climb()
-    to_owner(1)
-    for k in range(2, len(parts)):
-        to_sibling(k)
-    for k in direct[2:] + [swing]:
-        to_owner(k)
+    else:
+        to_owner(1)
+    if relayed:
+        tail_to_sibling()
+        to_sibling(swing)
+        to_owner(1)
+        tail_to_owner()
+        to_owner(swing)
+    else:
+        for k in range(2, len(parts)):
+            to_sibling(k)
+        for k in range(2, len(parts)):
+            to_owner(k)
 
     next_round()
     for k, (start, size) in enumerate(parts):
@@ -335,6 +378,8 @@
                         ring_recv.at[0, pl.ds(start, size)], ring_recv.at[0, pl.ds(start, size)],
                         rs_sem.at[0], rr_sem.at[swing, 0], device_id=across, device_id_type=MESH,
                     ).wait_recv()
+                elif relayed and k == tail:
+                    tail_copy(0).wait_recv()
                 else:
                     ring[k, slot].wait_recv()
             value = value + ring_recv[slot - 1, at, :]
@@ -382,17 +427,34 @@
         stats[i:i + 1, :] = row
 
     with jax.named_scope("send_wait"):
+        sent = pl.ds(0, parts[tail][0] if relayed else rows)
+        slots = pl.ds(0, chips - 1)
         pltpu.make_async_remote_copy(
-            pair_send, pair_recv, ps_sem.at[0], pr_sem.at[0], device_id=sibling, device_id_type=MESH
+            pair_send.at[0], pair_recv.at[0], ps_sem.at[0], pr_sem.at[0], device_id=sibling, device_id_type=MESH
         ).wait_send()
         kepts.wait_send()
         if far:
             pltpu.make_async_remote_copy(
-                ring_send, ring_recv, rs_sem.at[0], rr_sem.at[0, 0], device_id=sibling, device_id_type=MESH
+                ring_send.at[slots, sent], ring_recv.at[slots, sent], ps_sem.at[1], pr_sem.at[0],
+                device_id=sibling, device_id_type=MESH,
+            ).wait_send()
+            pltpu.make_async_remote_copy(
+                ring_send.at[slots, sent], ring_recv.at[slots, sent], rs_sem.at[0], rr_sem.at[0, 0],
+                device_id=sibling, device_id_type=MESH,
             ).wait_send()
         for copy in done:
             copy.wait_send()
         if relayed:
+            @pl.when(core == 0)
+            def _():
+                tail_pair().wait_send()
+
+            @pl.when(core == 1)
+            def _():
+                pltpu.make_async_remote_copy(
+                    tail_ring, tail_recv, tail_sem.at[1], tail_sem.at[0], device_id=sibling, device_id_type=MESH
+                ).wait_send()
+
             for h, taken in enumerate(borrow):
                 @pl.when(taken)
                 def _():
@@ -478,17 +540,21 @@
             pltpu.VMEM((n - 1, 1, padded), f32),
             [pltpu.VMEM((2, LANES), f32) for _ in peers],
             [pltpu.VMEM((max(size, 1), 2, LANES), f32) for size in peers],
-            pltpu.VMEM((PIECES - 1, 16, width // PIECES), f32),
+            pltpu.VMEM((PIECES - 1, 16, width // 2), f32),
+            pltpu.VMEM((2, 8, width), f32),
+            pltpu.VMEM((2, 8, width), f32),
+            pltpu.VMEM((2, 8, width), f32),
             dma((2,)),
             dma((len(cuts) - 1,)),
             dma((1,)),
-            dma((1,)),
+            dma((2,)),
             dma((len(cuts),)),
             dma((1,)),
             dma((len(cuts) - 1, others)),
             dma((2,)),
             dma((len(peers), 2)),
             dma((PIECES - 1,)),
+            dma((2,)),
             pltpu.SemaphoreType.REGULAR((3,)),
             pltpu.SemaphoreType.REGULAR((rounds,)),
         ],

time: 25.2 us -> 24.3 us (0.964)
  Pallas kernels: 23.8 us -> 22.8 us
    pallas_call x1, Pallas kernels: 22.3 us -> 21.3 us  [body(): pl.pallas_call(functools.partial(exchange, sizes, stages, cuts), out_shap...]
where the time goes in v3:
time: 24.3 us; the launch traced here: 24.1 us
  Pallas kernels  22.8 us (94%)
  between operations  1.29 us (5%)
    pallas_call x1, Pallas kernels, body(): pl.pallas_call(functools.partial(exchange, sizes, stages, cuts), out_shap...  21.3 us
    pallas_call x1, Pallas kernels, body(): pl.pallas_call(functools.partial(update, entries, chunks), out_shape=(sta...  1.48 us

profile of v3, /device:TPU:0, one launch (start us, length us, event | category | flops | bytes accessed | tf_op | source)
XLA Modules:
  0.0 24.1 jit_solution(415812693696105626)
XLA Ops:
  1.3 21.3 %shard_map.110 = (f32[64,2048]{1,0:T(8,128)S(1)}, f32[3,64,2048]{2,1,0:T(8,128)S(1)}, f32[24,128]{1,0:T(8,128)S(1)}) custom-call(s32[]{:T(128)S(6)} %copy.12.step_ref, s32[4]{0:T(128)} %order_hbm.1, s32[1,1,64]{2,1,0:T(1,128)} %bitcast.2, f32[1,1,1,64,8192]{4,3,2,1,0:T(8,128)} %grad_hbm.1, f32[1,1,64,2048]{3,2,1,0:T(8,128)} %w_hbm.1, ...), custom_call_target="tpu_custom_call" | custom-call | flops 4194304 | bytes 41943040 | tf_op jit(solution)/shard_map/pallas_call | solution.py:526
  22.6 1.5 %shard_map.111 = (f32[1,1,64,2048]{3,2,1,0:T(8,128)}, f32[1,1,64,2048]{3,2,1,0:T(8,128)}, f32[1,1,64,2048]{3,2,1,0:T(8,128)}, f32[1,1,64,2048]{3,2,1,0:T(8,128)}, s32[1]{0:T(128)}) custom-call(f32[24,128]{1,0:T(8,128)S(1)} %get-tuple-element.13.stats, f32[64,2048]{1,0:T(8,128)S(1)} %get-tuple-element.14.grad_ref, f32[3,64,2048]{2,1,0:T(8,128)S(1)} %get-tuple-element.15.held), custom_call_target="tpu_custom_call" | custom-call | flops 2621440 | bytes 4194304 | tf_op jit(solution)/shard_map/pallas_call | solution.py:568

commit v4 on v3

--- a/solution.py
+++ b/solution.py
@@ -42,7 +42,7 @@
     total, held, stats,
     order_ref, flags_ref, g_bufs, pair_send, pair_recv, ring_send, ring_recv,
     kept_send, kept_recv, red_sends, red_recvs,
-    relay_buf, tail_send, tail_recv, tail_ring, o_sem, g_sem, w_sem, ps_sem, pr_sem, rs_sem, rr_sem, k_sem, a_sem, via_sem, tail_sem, chain_sem, ready_sem,
+    step_send, step_recv, relay_buf, tail_send, tail_recv, tail_ring, o_sem, g_sem, w_sem, ps_sem, pr_sem, rs_sem, rr_sem, k_sem, a_sem, via_sem, step_sem, tail_sem, chain_sem, ready_sem,
 ):
     n = sizes["dp"]
     chips = n // 2
@@ -341,6 +341,7 @@
     for i in range(n - 1):
         count_row = count_row + kept_recv[i, :, 0:rows]
     inverse = 1.0 / jnp.maximum(as_column(count_row, rows), 1.0)
+    next_round()
     for i, source in enumerate((w_hbm, m_hbm, v_hbm)):
         pltpu.make_async_copy(source.at[0, 0], held.at[i], w_sem.at[0]).start()
 
@@ -353,10 +354,7 @@
     pltpu.make_async_copy(held, held, w_sem.at[0]).wait()
     held[1] = 0.9 * held[1]
     held[2] = 0.999 * held[2]
-    steps = jnp.full((SUBLANES, LANES), step_ref[...], jnp.int32)
-    stats[0:8, :] = jnp.zeros((SUBLANES, LANES), jnp.float32)
-    stats[8:16, :] = 1.0 / (1.0 - int_power(0.9, steps))
-    stats[16:24, :] = 1.0 / (1.0 - int_power(0.999, steps))
+    next_round()
 
     if relayed:
         for h in (2, 0, 1):
@@ -366,7 +364,22 @@
                     via_copy(h).wait_recv()
                 forward_copy(h).start()
 
-    per_part = -(-(len(rounds) + 1) // max(len(parts) - 1, 1))
+    while left or owed:
+        next_round()
+    first = functools.reduce(jnp.logical_and, [me[axis] == 0 for axis in stages[0]])
+
+    def tell(device):
+        return pltpu.make_async_remote_copy(
+            step_send, step_recv, step_sem.at[0], step_sem.at[1], device_id=device, device_id_type=MESH
+        )
+
+    @pl.when(first)
+    def _():
+        step_send[...] = step_ref[...]
+        step_recv[...] = step_ref[...]
+        for off in offsets_of(stages[0]):
+            tell(off).start()
+
     squares = jnp.zeros((SUBLANES, LANES), jnp.float32)
     for k, (start, size) in enumerate(parts):
         at = slice(start, start + size)
@@ -388,8 +401,6 @@
         squares = squares + jnp.sum(
             (value * value).reshape(size // SUBLANES, SUBLANES, width // LANES, LANES), axis=(0, 2)
         )
-        for _ in range(per_part):
-            next_round()
 
     result = [jnp.sum(squares, axis=0, keepdims=True), jnp.broadcast_to(dropped, (1, LANES))]
     done = []
@@ -415,6 +426,15 @@
                 @pl.when(back != i + 1)
                 def _():
                     share(i, peer(off))
+        if stage == 0:
+            @pl.when(jnp.logical_not(first))
+            def _():
+                tell(sibling).wait_recv()
+
+            steps = jnp.broadcast_to(step_recv[0:1, :], (SUBLANES, LANES)).astype(jnp.int32)
+            stats[0:8, :] = jnp.zeros((SUBLANES, LANES), jnp.float32)
+            stats[8:16, :] = 1.0 / (1.0 - int_power(0.9, steps))
+            stats[16:24, :] = 1.0 / (1.0 - int_power(0.999, steps))
         copy = pltpu.make_async_remote_copy(
             recv, recv, a_sem.at[stage, 0], a_sem.at[stage, 1], device_id=sibling, device_id_type=MESH
         )
@@ -444,6 +464,13 @@
             ).wait_send()
         for copy in done:
             copy.wait_send()
+
+        @pl.when(first)
+        def _():
+            pltpu.make_async_remote_copy(
+                red_recvs[0], red_recvs[0], step_sem.at[0], step_sem.at[1], device_id=sibling, device_id_type=MESH
+            ).wait_send()
+
         if relayed:
             @pl.when(core == 0)
             def _():
@@ -518,15 +545,20 @@
     f32 = jnp.float32
     dma = pltpu.SemaphoreType.DMA
     vmem = pl.BlockSpec(memory_space=pltpu.VMEM)
-    smem = pl.BlockSpec(memory_space=pltpu.SMEM)
     hbm = pl.BlockSpec(memory_space=pltpu.HBM)
     state = jax.ShapeDtypeStruct(master.shape, f32)
     block = rows * columns * 4
     inputs = (owner_order, drop_flags.reshape(drop_flags.shape[-3:]), grad_parts, master, moment_m, moment_v)
+    steps = lax.cond(
+        lax.axis_index(stages[0]) == 0,
+        lambda count: jnp.full((2, LANES), count.astype(f32)),
+        lambda count: jnp.zeros((2, LANES), f32),
+        step_count,
+    )
     total, held, stats = pl.pallas_call(
         functools.partial(exchange, sizes, stages, cuts),
         out_shape=tuple(pltpu.VMEM(shape, f32) for shape in ((rows, width), (3, rows, width), (3 * SUBLANES, LANES))),
-        in_specs=[smem] + [hbm] * 6,
+        in_specs=[vmem] + [hbm] * 6,
         out_specs=(vmem,) * 3,
         scratch_shapes=[
             pltpu.SMEM((n,), jnp.int32),
@@ -540,6 +572,8 @@
             pltpu.VMEM((n - 1, 1, padded), f32),
             [pltpu.VMEM((2, LANES), f32) for _ in peers],
             [pltpu.VMEM((max(size, 1), 2, LANES), f32) for size in peers],
+            pltpu.VMEM((2, LANES), f32),
+            pltpu.VMEM((2, LANES), f32),
             pltpu.VMEM((PIECES - 1, 16, width // 2), f32),
             pltpu.VMEM((2, 8, width), f32),
             pltpu.VMEM((2, 8, width), f32),
@@ -555,6 +589,7 @@
             dma((len(peers), 2)),
             dma((PIECES - 1,)),
             dma((2,)),
+            dma((2,)),
             pltpu.SemaphoreType.REGULAR((3,)),
             pltpu.SemaphoreType.REGULAR((rounds,)),
         ],
@@ -564,7 +599,7 @@
         cost_estimate=pl.CostEstimate(
             flops=8 * rows * columns, bytes_accessed=20 * rows * columns * 4, transcendentals=0
         ),
-    )(step_count, *(pltpu.with_memory_space_constraint(x, pltpu.HBM) for x in inputs))
+    )(pltpu.with_memory_space_constraint(steps, pltpu.VMEM), *(pltpu.with_memory_space_constraint(x, pltpu.HBM) for x in inputs))
     outs = pl.pallas_call(
         functools.partial(update, entries, chunks),
         out_shape=(state, state, state, state, jax.ShapeDtypeStruct((1,), jnp.int32)),

time: 24.3 us -> 23.7 us (0.975)
  loops' own time: 0 us -> 0.67 us
  between operations: 1.29 us -> 0.66 us
  Pallas kernels: 22.8 us -> 22.2 us
    another operation x0 -> x1, loops' own time: none -> 0.67 us  [body(): lax.cond(lax.axis_index(stages[0]) == 0, lambda count: jnp.full((2, LANES...]
    pallas_call x1, Pallas kernels: 21.3 us -> 20.7 us  [body(): pl.pallas_call(functools.partial(exchange, sizes, stages, cuts), out_shap...]
where the time goes in v4:
time: 23.7 us; the launch traced here: 23.5 us
  Pallas kernels  22.2 us (94%)
  loops' own time  0.67 us (3%)
  between operations  0.66 us (3%)
    pallas_call x1, Pallas kernels, body(): pl.pallas_call(functools.partial(exchange, sizes, stages, cuts), out_shap...  20.7 us
    pallas_call x1, Pallas kernels, body(): pl.pallas_call(functools.partial(update, entries, chunks), out_shape=(sta...  1.48 us
    another operation x1, loops' own time, body(): lax.cond(lax.axis_index(stages[0]) == 0, lambda count: jnp.full((2, LANES...  0.67 us

profile of v4, /device:TPU:0, one launch (start us, length us, event | category | flops | bytes accessed | tf_op | source)
XLA Modules:
  0.0 23.5 jit_solution(17800121938175583167)
XLA Ops:
  0.6 0.7 %conditional.1 = (f32[2,128]{1,0:T(2,128)S(1)}) conditional(s32[]{:T(128)} %convert_element_type.6, () %tuple.14, (s32[]{:T(128)}) %tuple.16), branch_computations={%region_0.0_spmd, %region_1.0_spmd} | conditional | flops 1 | bytes 1044 | solution.py:552
  1.3 20.7 %shard_map.114 = (f32[64,2048]{1,0:T(8,128)S(1)}, f32[3,64,2048]{2,1,0:T(8,128)S(1)}, f32[24,128]{1,0:T(8,128)S(1)}) custom-call(f32[2,128]{1,0:T(2,128)S(1)} %get-tuple-element.27.step_ref, s32[4]{0:T(128)} %order_hbm.1, s32[1,1,64]{2,1,0:T(1,128)} %bitcast.2, f32[1,1,1,64,8192]{4,3,2,1,0:T(8,128)} %grad_hbm.1, f32[1,1,64,2048]{3,2,1,0:T(8,128)} %w_hbm.1, ...), custom_call_target="tpu_custom_call" | custom-call | flops 4194304 | bytes 41943040 | tf_op jit(solution)/shard_map/pallas_call | solution.py:558
  22.0 1.5 %shard_map.115 = (f32[1,1,64,2048]{3,2,1,0:T(8,128)}, f32[1,1,64,2048]{3,2,1,0:T(8,128)}, f32[1,1,64,2048]{3,2,1,0:T(8,128)}, f32[1,1,64,2048]{3,2,1,0:T(8,128)}, s32[1]{0:T(128)}) custom-call(f32[24,128]{1,0:T(8,128)S(1)} %get-tuple-element.17.stats, f32[64,2048]{1,0:T(8,128)S(1)} %get-tuple-element.18.grad_ref, f32[3,64,2048]{2,1,0:T(8,128)S(1)} %get-tuple-element.19.held), custom_call_target="tpu_custom_call" | custom-call | flops 2621440 | bytes 4194304 | tf_op jit(solution)/shard_map/pallas_call | solution.py:603
  (1 shorter events, 0.0 us)

commit v5 on v4

--- a/solution.py
+++ b/solution.py
@@ -42,7 +42,8 @@
     total, held, stats,
     order_ref, flags_ref, g_bufs, pair_send, pair_recv, ring_send, ring_recv,
     kept_send, kept_recv, red_sends, red_recvs,
-    step_send, step_recv, relay_buf, tail_send, tail_recv, tail_ring, o_sem, g_sem, w_sem, ps_sem, pr_sem, rs_sem, rr_sem, k_sem, a_sem, via_sem, step_sem, tail_sem, chain_sem, ready_sem,
+    step_send, step_recv, relay_buf, tail_send, tail_recv, tail_ring,
+    o_sem, g_sem, pr_sem, rr_sem, k_sem, a_sem, via_sem, step_sem, tail_sem, chain_sem, ready_sem,
 ):
     n = sizes["dp"]
     chips = n // 2
@@ -59,6 +60,8 @@
         ranges = [range(sizes[axis]) for axis in axes]
         return [dict(zip(axes, offs)) for offs in itertools.product(*ranges) if any(offs)]
 
+    pair_sent, row_sent = o_sem.at[0], o_sem.at[1]
+    ring_sent, tail_sent, held_sem, tail_paired = (g_sem.at[i] for i in range(4))
     small = [
         pltpu.make_async_copy(flags_hbm, flags_ref, o_sem.at[0]),
         pltpu.make_async_copy(order_hbm, order_ref, o_sem.at[1]),
@@ -152,7 +155,7 @@
     def send_pair(k, slot):
         copy = pltpu.make_async_remote_copy(
             rows_of(pair_send, slot, k), rows_of(pair_recv, slot, k),
-            ps_sem.at[1 if slot else 0], pr_sem.at[k if slot else len(parts)],
+            pair_sent, pr_sem.at[k if slot else pr_sem.shape[0] - 1],
             device_id=sibling, device_id_type=MESH,
         )
         copy.start()
@@ -174,7 +177,7 @@
             send_pair(k, slot)
 
     kepts = pltpu.make_async_remote_copy(
-        kept_recv, kept_recv, k_sem.at[0], k_sem.at[1], device_id=sibling, device_id_type=MESH
+        kept_recv, kept_recv, row_sent, k_sem.at[0], device_id=sibling, device_id_type=MESH
     )
 
     ring = {}
@@ -196,13 +199,13 @@
 
     def swing_copy(h):
         return pltpu.make_async_remote_copy(
-            piece(ring_send, h), piece(ring_recv, h), rs_sem.at[0], rr_sem.at[swing, 0],
+            piece(ring_send, h), piece(ring_recv, h), ring_sent, rr_sem.at[swing, 0],
             device_id=across, device_id_type=MESH,
         )
 
     def via_copy(h):
         return pltpu.make_async_remote_copy(
-            piece(ring_send, h), lodging(h), rs_sem.at[0], via_sem.at[h],
+            piece(ring_send, h), lodging(h), ring_sent, via_sem.at[h],
             device_id={**across, **mirror[h]}, device_id_type=MESH,
         )
 
@@ -233,12 +236,12 @@
 
     def tail_pair():
         return pltpu.make_async_remote_copy(
-            tail_send, tail_recv, tail_sem.at[0], tail_sem.at[0], device_id=sibling, device_id_type=MESH
+            tail_send, tail_recv, tail_paired, tail_sem.at[0], device_id=sibling, device_id_type=MESH
         )
 
     def tail_copy(c):
         return pltpu.make_async_remote_copy(
-            tail_ring.at[c], ring_recv.at[0, tail_at], tail_sem.at[1], rr_sem.at[tail, 0],
+            tail_ring.at[c], ring_recv.at[0, tail_at], tail_sent, rr_sem.at[tail, 0],
             device_id={"dp": abroad + c}, device_id_type=MESH,
         )
 
@@ -269,7 +272,7 @@
                     pltpu.make_async_remote_copy(
                         pair_recv.at[pl.ds(1, chips - 1), pl.ds(start, size)],
                         pair_recv.at[pl.ds(1, chips - 1), pl.ds(start, size)],
-                        ps_sem.at[0], pr_sem.at[k], device_id=sibling, device_id_type=MESH,
+                        pair_sent, pr_sem.at[k], device_id=sibling, device_id_type=MESH,
                     ).wait_recv()
             ring_send[slot - 1, start:start + size, :] = pair_recv[slot, start:start + size, :] + mine
             if relayed and k == swing:
@@ -292,7 +295,7 @@
                 continue
             copy = pltpu.make_async_remote_copy(
                 rows_of(ring_send, slot - 1, k), rows_of(ring_recv, slot - 1, k),
-                rs_sem.at[0], rr_sem.at[k, slot - 1],
+                ring_sent, rr_sem.at[k, slot - 1],
                 device_id={"dp": target}, device_id_type=MESH,
             )
             copy.start()
@@ -311,7 +314,7 @@
             pl.semaphore_wait(chain_sem.at[2], 1)
     for off in range(1, n):
         pltpu.make_async_remote_copy(
-            kept_send.at[0], kept_recv.at[off - 1], k_sem.at[0], k_sem.at[1],
+            kept_send.at[0], kept_recv.at[off - 1], row_sent, k_sem.at[0],
             device_id=peer({"dp": off}), device_id_type=MESH,
         ).start()
     to_owner(0)
@@ -332,26 +335,34 @@
             to_owner(k)
 
     next_round()
+    sent = pl.ds(0, parts[tail][0] if relayed else rows)
+    slots = pl.ds(0, chips - 1)
+    if far:
+        pltpu.make_async_remote_copy(
+            ring_send.at[slots, sent], ring_recv.at[slots, sent], pair_sent, pr_sem.at[0],
+            device_id=sibling, device_id_type=MESH,
+        ).wait_send()
     for k, (start, size) in enumerate(parts):
         pair_send[0, start:start + size, :] = term(k, chip * 2 + 1 - core)
         send_pair(k, 0)
     with jax.named_scope("kept_wait"):
         kepts.wait_recv()
+    kepts.wait_send()
     count_row = kept_row
     for i in range(n - 1):
         count_row = count_row + kept_recv[i, :, 0:rows]
     inverse = 1.0 / jnp.maximum(as_column(count_row, rows), 1.0)
     next_round()
     for i, source in enumerate((w_hbm, m_hbm, v_hbm)):
-        pltpu.make_async_copy(source.at[0, 0], held.at[i], w_sem.at[0]).start()
+        pltpu.make_async_copy(source.at[0, 0], held.at[i], held_sem).start()
 
     pltpu.make_async_remote_copy(
-        pair_recv.at[0], pair_recv.at[0], ps_sem.at[0], pr_sem.at[len(parts)],
+        pair_recv.at[0], pair_recv.at[0], pair_sent, pr_sem.at[pr_sem.shape[0] - 1],
         device_id=sibling, device_id_type=MESH,
     ).wait_recv()
     for k, (start, size) in enumerate(parts):
         total[start:start + size, :] = pair_recv[0, start:start + size, :] + term(k, me["dp"])
-    pltpu.make_async_copy(held, held, w_sem.at[0]).wait()
+    pltpu.make_async_copy(held, held, held_sem).wait()
     held[1] = 0.9 * held[1]
     held[2] = 0.999 * held[2]
     next_round()
@@ -370,7 +381,7 @@
 
     def tell(device):
         return pltpu.make_async_remote_copy(
-            step_send, step_recv, step_sem.at[0], step_sem.at[1], device_id=device, device_id_type=MESH
+            step_send, step_recv, row_sent, step_sem.at[0], device_id=device, device_id_type=MESH
         )
 
     @pl.when(first)
@@ -381,7 +392,8 @@
             tell(off).start()
 
     squares = jnp.zeros((SUBLANES, LANES), jnp.float32)
-    for k, (start, size) in enumerate(parts):
+    for k in [i for i in range(len(parts)) if not relayed or i != swing] + [swing] * relayed:
+        start, size = parts[k]
         at = slice(start, start + size)
         value = total[at, :]
         for slot in far:
@@ -389,7 +401,7 @@
                 if relayed and k == swing:
                     pltpu.make_async_remote_copy(
                         ring_recv.at[0, pl.ds(start, size)], ring_recv.at[0, pl.ds(start, size)],
-                        rs_sem.at[0], rr_sem.at[swing, 0], device_id=across, device_id_type=MESH,
+                        ring_sent, rr_sem.at[swing, 0], device_id=across, device_id_type=MESH,
                     ).wait_recv()
                 elif relayed and k == tail:
                     tail_copy(0).wait_recv()
@@ -402,8 +414,13 @@
             (value * value).reshape(size // SUBLANES, SUBLANES, width // LANES, LANES), axis=(0, 2)
         )
 
+    @pl.when(first)
+    def _():
+        pltpu.make_async_remote_copy(
+            red_recvs[0], red_recvs[0], row_sent, step_sem.at[0], device_id=sibling, device_id_type=MESH
+        ).wait_send()
+
     result = [jnp.sum(squares, axis=0, keepdims=True), jnp.broadcast_to(dropped, (1, LANES))]
-    done = []
     for stage, (axes, send, recv) in enumerate(zip(stages, red_sends, red_recvs)):
         for i, row in enumerate(result):
             send[i:i + 1, :] = row
@@ -414,7 +431,7 @@
 
             def share(i, device):
                 pltpu.make_async_remote_copy(
-                    send, recv.at[i], a_sem.at[stage, 0], a_sem.at[stage, 1],
+                    send, recv.at[i], row_sent, a_sem.at[stage],
                     device_id=device, device_id_type=MESH,
                 ).start()
 
@@ -436,41 +453,25 @@
             stats[8:16, :] = 1.0 / (1.0 - int_power(0.9, steps))
             stats[16:24, :] = 1.0 / (1.0 - int_power(0.999, steps))
         copy = pltpu.make_async_remote_copy(
-            recv, recv, a_sem.at[stage, 0], a_sem.at[stage, 1], device_id=sibling, device_id_type=MESH
-        )
-        done.append(copy)
+            recv, recv, row_sent, a_sem.at[stage], device_id=sibling, device_id_type=MESH
+        )
         with jax.named_scope("norm_wait"):
             copy.wait_recv()
+        copy.wait_send()
         for i in range(len(offsets_of(axes))):
             result = [row + recv[i, j:j + 1, :] for j, row in enumerate(result)]
     for i, row in enumerate(result):
         stats[i:i + 1, :] = row
 
     with jax.named_scope("send_wait"):
-        sent = pl.ds(0, parts[tail][0] if relayed else rows)
-        slots = pl.ds(0, chips - 1)
         pltpu.make_async_remote_copy(
-            pair_send.at[0], pair_recv.at[0], ps_sem.at[0], pr_sem.at[0], device_id=sibling, device_id_type=MESH
+            pair_send.at[0], pair_recv.at[0], pair_sent, pr_sem.at[0], device_id=sibling, device_id_type=MESH
         ).wait_send()
-        kepts.wait_send()
         if far:
             pltpu.make_async_remote_copy(
-                ring_send.at[slots, sent], ring_recv.at[slots, sent], ps_sem.at[1], pr_sem.at[0],
+                ring_send.at[slots, sent], ring_recv.at[slots, sent], ring_sent, rr_sem.at[0, 0],
                 device_id=sibling, device_id_type=MESH,
             ).wait_send()
-            pltpu.make_async_remote_copy(
-                ring_send.at[slots, sent], ring_recv.at[slots, sent], rs_sem.at[0], rr_sem.at[0, 0],
-                device_id=sibling, device_id_type=MESH,
-            ).wait_send()
-        for copy in done:
-            copy.wait_send()
-
-        @pl.when(first)
-        def _():
-            pltpu.make_async_remote_copy(
-                red_recvs[0], red_recvs[0], step_sem.at[0], step_sem.at[1], device_id=sibling, device_id_type=MESH
-            ).wait_send()
-
         if relayed:
             @pl.when(core == 0)
             def _():
@@ -479,7 +480,7 @@
             @pl.when(core == 1)
             def _():
                 pltpu.make_async_remote_copy(
-                    tail_ring, tail_recv, tail_sem.at[1], tail_sem.at[0], device_id=sibling, device_id_type=MESH
+                    tail_ring, tail_recv, tail_sent, tail_sem.at[0], device_id=sibling, device_id_type=MESH
                 ).wait_send()
 
             for h, taken in enumerate(borrow):
@@ -501,19 +502,25 @@
     clip = jnp.minimum(1.0, 0.05 / (rms + 1e-06))
     share_m, share_v = 0.1 * clip, math.sqrt(0.001) * clip
     outs = (w_out, m_out, v_out, dir_out)
+
+    def put(i, k, value):
+        bufs[i, k * part:(k + 1) * part, :] = value
+        rows_of = pl.ds(k * part, part)
+        pltpu.make_async_copy(bufs.at[i, rows_of], outs[i].at[0, 0, rows_of], sems.at[i]).start()
+
     for k in range(chunks):
         at = slice(k * part, (k + 1) * part)
         grad = grad_ref[at, :]
         root = grad * share_v
-        new_m = held[1, at, :] + grad * share_m
-        new_v = held[2, at, :] + root * root
+        put(1, k, held[1, at, :] + grad * share_m)
+        put(2, k, held[2, at, :] + root * root)
+    for k in range(chunks):
+        at = slice(k * part, (k + 1) * part)
         weights = held[0, at, :]
-        corrected = new_v * scale_v
-        direction = (new_m * scale_m) / (corrected * lax.rsqrt(corrected) + 1e-08) + 0.1 * weights
-        values = (weights - 0.001 * direction, new_m, new_v, direction)
-        for i, (value, out) in enumerate(zip(values, outs)):
-            bufs[i, at, :] = value
-            pltpu.make_async_copy(bufs.at[i, pl.ds(k * part, part)], out.at[0, 0, pl.ds(k * part, part)], sems.at[i]).start()
+        corrected = bufs[2, at, :] * scale_v
+        direction = (bufs[1, at, :] * scale_m) / (corrected * lax.rsqrt(corrected) + 1e-08) + 0.1 * weights
+        put(3, k, direction)
+        put(0, k, weights - 0.001 * direction)
         if k == 0:
             drop_ref[0] = jnp.max(stats[1:2, :]).astype(jnp.int32)
             drop = pltpu.make_async_copy(drop_ref, drop_out, sems.at[4])
@@ -579,17 +586,14 @@
             pltpu.VMEM((2, 8, width), f32),
             pltpu.VMEM((2, 8, width), f32),
             dma((2,)),
-            dma((len(cuts) - 1,)),
+            dma((max(len(cuts) - 1, 4),)),
+            dma((len(cuts) - 1 if can_relay(sizes, stages) else len(cuts),)),
+            dma((len(cuts) - 1, others)),
             dma((1,)),
-            dma((2,)),
-            dma((len(cuts),)),
+            dma((len(peers),)),
+            dma((PIECES - 1,)),
             dma((1,)),
-            dma((len(cuts) - 1, others)),
-            dma((2,)),
-            dma((len(peers), 2)),
-            dma((PIECES - 1,)),
-            dma((2,)),
-            dma((2,)),
+            dma((1,)),
             pltpu.SemaphoreType.REGULAR((3,)),
             pltpu.SemaphoreType.REGULAR((rounds,)),
         ],

time: 23.7 us -> 23.5 us (level)
  no operation moved by 1% of the time
where the time goes in v5:
time: 23.5 us; the launch traced here: 23.4 us
  Pallas kernels  22 us (94%)
  loops' own time  0.67 us (3%)
  between operations  0.66 us (3%)
    pallas_call x1, Pallas kernels, body(): pl.pallas_call(functools.partial(exchange, sizes, stages, cuts), out_shap...  20.6 us
    pallas_call x1, Pallas kernels, body(): pl.pallas_call(functools.partial(update, entries, chunks), out_shape=(sta...  1.45 us
    another operation x1, loops' own time, body(): lax.cond(lax.axis_index(stages[0]) == 0, lambda count: jnp.full((2, LANES...  0.67 us

profile of v5, /device:TPU:0, one launch (start us, length us, event | category | flops | bytes accessed | tf_op | source)
XLA Modules:
  0.0 23.4 jit_solution(7584411109712090307)
XLA Ops:
  0.6 0.7 %conditional.1 = (f32[2,128]{1,0:T(2,128)S(1)}) conditional(s32[]{:T(128)} %convert_element_type.6, () %tuple.14, (s32[]{:T(128)}) %tuple.16), branch_computations={%region_0.0_spmd, %region_1.0_spmd} | conditional | flops 1 | bytes 1044 | solution.py:559
  1.3 20.6 %shard_map.114 = (f32[64,2048]{1,0:T(8,128)S(1)}, f32[3,64,2048]{2,1,0:T(8,128)S(1)}, f32[24,128]{1,0:T(8,128)S(1)}) custom-call(f32[2,128]{1,0:T(2,128)S(1)} %get-tuple-element.27.step_ref, s32[4]{0:T(128)} %order_hbm.1, s32[1,1,64]{2,1,0:T(1,128)} %bitcast.2, f32[1,1,1,64,8192]{4,3,2,1,0:T(8,128)} %grad_hbm.1, f32[1,1,64,2048]{3,2,1,0:T(8,128)} %w_hbm.1, ...), custom_call_target="tpu_custom_call" | custom-call | flops 4194304 | bytes 41943040 | tf_op jit(solution)/shard_map/pallas_call | solution.py:565
  21.9 1.4 %shard_map.115 = (f32[1,1,64,2048]{3,2,1,0:T(8,128)}, f32[1,1,64,2048]{3,2,1,0:T(8,128)}, f32[1,1,64,2048]{3,2,1,0:T(8,128)}, f32[1,1,64,2048]{3,2,1,0:T(8,128)}, s32[1]{0:T(128)}) custom-call(f32[24,128]{1,0:T(8,128)S(1)} %get-tuple-element.17.stats, f32[64,2048]{1,0:T(8,128)S(1)} %get-tuple-element.18.grad_ref, f32[3,64,2048]{2,1,0:T(8,128)S(1)} %get-tuple-element.19.held), custom_call_target="tpu_custom_call" | custom-call | flops 2621440 | bytes 4194304 | tf_op jit(solution)/shard_map/pallas_call | solution.py:607
  (1 shorter events, 0.0 us)

commit v6 on v5

--- a/solution.py
+++ b/solution.py
@@ -323,8 +323,8 @@
     else:
         to_owner(1)
     if relayed:
+        to_sibling(swing)
         tail_to_sibling()
-        to_sibling(swing)
         to_owner(1)
         tail_to_owner()
         to_owner(swing)
@@ -458,8 +458,11 @@
         with jax.named_scope("norm_wait"):
             copy.wait_recv()
         copy.wait_send()
-        for i in range(len(offsets_of(axes))):
-            result = [row + recv[i, j:j + 1, :] for j, row in enumerate(result)]
+        chains = [jnp.concatenate(result, axis=0)] + [recv[i] for i in range(min(3, recv.shape[0]))]
+        for i in range(3, len(offsets_of(axes))):
+            chains[i % 4] = chains[i % 4] + recv[i]
+        both = functools.reduce(jnp.add, chains[:1 + len(offsets_of(axes))])
+        result = [both[0:1], both[1:2]]
     for i, row in enumerate(result):
         stats[i:i + 1, :] = row
 

time: 23.5 us -> 23.5 us (level)
  no operation moved by 1% of the time
where the time goes in v6:
time: 23.5 us; the launch traced here: 23.4 us
  Pallas kernels  22 us (94%)
  loops' own time  0.67 us (3%)
  between operations  0.66 us (3%)
    pallas_call x1, Pallas kernels, body(): pl.pallas_call(functools.partial(exchange, sizes, stages, cuts), out_shap...  20.6 us
    pallas_call x1, Pallas kernels, body(): pl.pallas_call(functools.partial(update, entries, chunks), out_shape=(sta...  1.45 us
    another operation x1, loops' own time, body(): lax.cond(lax.axis_index(stages[0]) == 0, lambda count: jnp.full((2, LANES...  0.67 us

profile of v6, /device:TPU:0, one launch (start us, length us, event | category | flops | bytes accessed | tf_op | source)
XLA Modules:
  0.0 23.4 jit_solution(350602064191140607)
XLA Ops:
  0.6 0.7 %conditional.1 = (f32[2,128]{1,0:T(2,128)S(1)}) conditional(s32[]{:T(128)} %convert_element_type.6, () %tuple.14, (s32[]{:T(128)}) %tuple.16), branch_computations={%region_0.0_spmd, %region_1.0_spmd} | conditional | flops 1 | bytes 1044 | solution.py:562
  1.3 20.6 %shard_map.114 = (f32[64,2048]{1,0:T(8,128)S(1)}, f32[3,64,2048]{2,1,0:T(8,128)S(1)}, f32[24,128]{1,0:T(8,128)S(1)}) custom-call(f32[2,128]{1,0:T(2,128)S(1)} %get-tuple-element.27.step_ref, s32[4]{0:T(128)} %order_hbm.1, s32[1,1,64]{2,1,0:T(1,128)} %bitcast.2, f32[1,1,1,64,8192]{4,3,2,1,0:T(8,128)} %grad_hbm.1, f32[1,1,64,2048]{3,2,1,0:T(8,128)} %w_hbm.1, ...), custom_call_target="tpu_custom_call" | custom-call | flops 4194304 | bytes 41943040 | tf_op jit(solution)/shard_map/pallas_call | solution.py:568
  21.9 1.4 %shard_map.115 = (f32[1,1,64,2048]{3,2,1,0:T(8,128)}, f32[1,1,64,2048]{3,2,1,0:T(8,128)}, f32[1,1,64,2048]{3,2,1,0:T(8,128)}, f32[1,1,64,2048]{3,2,1,0:T(8,128)}, s32[1]{0:T(128)}) custom-call(f32[24,128]{1,0:T(8,128)S(1)} %get-tuple-element.17.stats, f32[64,2048]{1,0:T(8,128)S(1)} %get-tuple-element.18.grad_ref, f32[3,64,2048]{2,1,0:T(8,128)S(1)} %get-tuple-element.19.held), custom_call_target="tpu_custom_call" | custom-call | flops 2621440 | bytes 4194304 | tf_op jit(solution)/shard_map/pallas_call | solution.py:610
  (1 shorter events, 0.0 us)

commit v7 on v6

--- a/solution.py
+++ b/solution.py
@@ -281,7 +281,7 @@
                     with jax.named_scope("chain_wait"):
                         pl.semaphore_wait(chain_sem.at[1], 1)
 
-                for h, away in enumerate(lend):
+                for h, away in ((1, lend[1]), (0, lend[0]), (2, lend[2])):
                     @pl.when(away)
                     def _():
                         via_copy(h).start()
@@ -368,7 +368,7 @@
     next_round()
 
     if relayed:
-        for h in (2, 0, 1):
+        for h in (2, 1, 0):
             @pl.when(borrow[h])
             def _():
                 with jax.named_scope(f"relay_wait{h}"):

time: 23.5 us -> 23.5 us (level)
  no operation moved by 1% of the time
where the time goes in v7:
time: 23.5 us; the launch traced here: 23.4 us
  Pallas kernels  22 us (94%)
  loops' own time  0.67 us (3%)
  between operations  0.66 us (3%)
    pallas_call x1, Pallas kernels, body(): pl.pallas_call(functools.partial(exchange, sizes, stages, cuts), out_shap...  20.6 us
    pallas_call x1, Pallas kernels, body(): pl.pallas_call(functools.partial(update, entries, chunks), out_shape=(sta...  1.45 us
    another operation x1, loops' own time, body(): lax.cond(lax.axis_index(stages[0]) == 0, lambda count: jnp.full((2, LANES...  0.67 us

profile of v7, /device:TPU:0, one launch (start us, length us, event | category | flops | bytes accessed | tf_op | source)
XLA Modules:
  0.0 23.4 jit_solution(4767651537416071412)
XLA Ops:
  0.6 0.7 %conditional.1 = (f32[2,128]{1,0:T(2,128)S(1)}) conditional(s32[]{:T(128)} %convert_element_type.6, () %tuple.14, (s32[]{:T(128)}) %tuple.16), branch_computations={%region_0.0_spmd, %region_1.0_spmd} | conditional | flops 1 | bytes 1044 | solution.py:562
  1.3 20.6 %shard_map.114 = (f32[64,2048]{1,0:T(8,128)S(1)}, f32[3,64,2048]{2,1,0:T(8,128)S(1)}, f32[24,128]{1,0:T(8,128)S(1)}) custom-call(f32[2,128]{1,0:T(2,128)S(1)} %get-tuple-element.27.step_ref, s32[4]{0:T(128)} %order_hbm.1, s32[1,1,64]{2,1,0:T(1,128)} %bitcast.2, f32[1,1,1,64,8192]{4,3,2,1,0:T(8,128)} %grad_hbm.1, f32[1,1,64,2048]{3,2,1,0:T(8,128)} %w_hbm.1, ...), custom_call_target="tpu_custom_call" | custom-call | flops 4194304 | bytes 41943040 | tf_op jit(solution)/shard_map/pallas_call | solution.py:568
  21.9 1.4 %shard_map.115 = (f32[1,1,64,2048]{3,2,1,0:T(8,128)}, f32[1,1,64,2048]{3,2,1,0:T(8,128)}, f32[1,1,64,2048]{3,2,1,0:T(8,128)}, f32[1,1,64,2048]{3,2,1,0:T(8,128)}, s32[1]{0:T(128)}) custom-call(f32[24,128]{1,0:T(8,128)S(1)} %get-tuple-element.17.stats, f32[64,2048]{1,0:T(8,128)S(1)} %get-tuple-element.18.grad_ref, f32[3,64,2048]{2,1,0:T(8,128)S(1)} %get-tuple-element.19.held), custom_call_target="tpu_custom_call" | custom-call | flops 2621440 | bytes 4194304 | tf_op jit(solution)/shard_map/pallas_call | solution.py:610
  (1 shorter events, 0.0 us)
